TPU v7x, 32 devices: a whole 2x2x4 slice. The times are simulated.
32 devices in a mesh: gy: 8 (over z, y), gz: 4 (over x, core).
Axes of the slice: x: 2, y: 2, z: 4, core: 2. Of those that a mesh axis runs over, the one named last changes fastest.
Arguments:
- wavefunction: float32 [2, 8, 1024, 1024], P(None, None, 'gy', 'gz'), may hold values from -6 to 6
- absorber: float32 [8, 1024, 1024], P(None, 'gy', 'gz'), may hold values from 0.05 to 1.5
- row_inverse: float32 [2, 1024, 128], P(None, 'gy'), may hold values from -1 to 1
- column_inverse: float32 [2, 1024, 256], replicated, may hold values from -1 to 1
- link_terms: float32 [2, 2, 2], replicated, may hold values from 0.65 to 0.7
- shell_blocks: int32 [4, 8, 56], P('gz'), may hold values from 0 to 63, as said below
- owner_map: int32 [4, 8, 56, 1], P('gz'), may hold values from 0 to 7; in each aligned block of 56 rows (0 to 55, 56 to 111, ..., all dimensions but the last counted through in order) at most 14 rows name the same one
- volkov_phase: float32 [128, 128], replicated, may hold values from -3.140625 to 3.140625
Outputs:
- damped: float32 [2, 8, 1024, 1024], P(None, None, 'gy', 'gz')
- spectrum: float32 [2, 64, 512, 128], P(None, 'gy', 'gz')
Inputs may be any that keep to these rules, and one draw needn't show every extreme that they name: `shell_blocks`: the ids listed for one device are distinct. `owner_map`: at most 14 of one device's listed blocks name the same owner.
All inputs are finite; a program needn't handle non-finite values.
Results may differ from a plain program's by a relative error of at most 0.0003.
Values sent between devices are 32-bit elements; how exact they have to be, the bound alone decides.
No kernel may reach another device: no remote copies, remote signals or barrier semaphores. Data moves between devices by JAX's collectives and lax.ppermute only.
A program may use at most 64 MiB of HBM per device.

v0:
```python
import math

import jax
import jax.numpy as jnp
import numpy as np
from jax import lax
from jax.experimental import pallas as pl
from jax.experimental.pallas import tpu as pltpu
from jax.sharding import PartitionSpec as P


BY = 2
KY = 128
KZ = 128
EDGE = 8
MBLOCK = 4

f32 = jnp.float32
bf16 = jnp.bfloat16
NN = (((1,), (0,)), ((), ()))
NT = (((1,), (1,)), ((), ()))
TN = (((0,), (0,)), ((), ()))


def mm(a, b, dims=NN):
    return lax.dot_general(a, b, dims, preferred_element_type=f32)


def split(a):
    hi = a.astype(bf16)
    return hi, (a - hi.astype(f32)).astype(bf16)


def mm3(a, b, dims=NN):
    return mm(a[0], b[0], dims) + mm(a[0], b[1], dims) + mm(a[1], b[0], dims)


def cmul(a, b):
    return (a[0] * b[0] - a[1] * b[1], a[0] * b[1] + a[1] * b[0])


def cdiv(a, b):
    modulus = b[0] * b[0] + b[1] * b[1]
    return ((a[0] * b[0] + a[1] * b[1]) / modulus, (a[1] * b[0] - a[0] * b[1]) / modulus)


def cadd(a, b):
    return (a[0] + b[0], a[1] + b[1])


def put(hi_ref, lo_ref, rows, cols, value):
    hi, lo = split(value)
    hi_ref[rows, cols] = hi
    lo_ref[rows, cols] = lo


def spikes_of(transposed, link, sweep):
    last = transposed[0].shape[0] - 1
    left = cmul(
        (link[sweep, 0, 0], link[sweep, 0, 1]), (transposed[0][0:1], transposed[1][0:1])
    )
    right = cmul(
        (link[sweep, 1, 0], link[sweep, 1, 1]),
        (transposed[0][last : last + 1], transposed[1][last : last + 1]),
    )
    return left, right


def edge_rows(left, right, lanes):
    last = left[0].shape[1] - 1
    rows = []
    for spike in (left, right):
        for at in (0, last):
            for part in spike:
                rows.append(jnp.broadcast_to(part[:, at : at + 1], (1, lanes)))
    return rows


VM = pl.BlockSpec(memory_space=pltpu.VMEM)
SM = pl.BlockSpec(memory_space=pltpu.SMEM)
AN = pl.BlockSpec(memory_space=pl.ANY)
LIMIT = pltpu.CompilerParams(vmem_limit_bytes=20 << 20)


def far(*values):
    return [pltpu.with_memory_space_constraint(value, pltpu.HBM) for value in values]


def paired_by_bits(groups):
    return groups & (groups - 1) == 0


def slot_of(owner, me, groups):
    return owner ^ me if paired_by_bits(groups) else (owner - me + groups) % groups


def source_of(step, me, groups):
    return me ^ step if paired_by_bits(groups) else (me - step + groups) % groups


def exchange(value, step, groups, axis="gy"):
    pairs = [
        (i, i ^ step if paired_by_bits(groups) else (i + step) % groups) for i in range(groups)
    ]
    return lax.ppermute(value, axis, pairs)


def inner_of(groups):
    bits = groups.bit_length() - 1
    return 1 << (bits // 2)


def row_edges_kernel(
    link, w, y, col, listed, owners, ps, spk, wv, yv, zv, iv, ov, sums, sems, ysem, zsems
):
    nx, n, width = wv.shape[1:]
    ycopy = pltpu.make_async_copy(y, yv, ysem)
    ycopy.start()
    copies = []
    for x in range(nx):
        copies.append(pltpu.make_async_copy(w.at[:, x], wv.at[:, x], sems.at[x]))
        copies[x].start()
    wz = zv.shape[1]
    rank = lax.axis_index("gz")
    loads = [
        pltpu.make_async_copy(col.at[:, pl.ds(rank * wz, wz), :], zv, zsems.at[0]),
        pltpu.make_async_copy(listed, iv, zsems.at[1]),
        pltpu.make_async_copy(owners, ov, zsems.at[2]),
    ]
    for load in loads:
        load.start()
    ycopy.wait()
    rt = yv[0].T
    it = yv[1].T
    left, right = spikes_of((rt, it), link, 0)
    for at, row in enumerate((left[0], left[1], right[0], right[1])):
        spk[at : at + 1, :] = row
    spk[4:8, :] = jnp.zeros((4, n), f32)
    lanes = ps.shape[2]
    count = width // lanes * nx
    for at, row in enumerate(edge_rows(left, right, lanes)):
        ps[0, 4 * count + at : 4 * count + at + 1, :] = row
    coef = [
        (
            jnp.broadcast_to(rt[:, row : row + 1], (n, lanes)),
            jnp.broadcast_to(it[:, row : row + 1], (n, lanes)),
        )
        for row in (0, n - 1)
    ]
    for x in range(nx):
        copies[x].wait()
        for k in range(width // lanes):
            cols = slice(k * lanes, (k + 1) * lanes)
            wr = wv[0, x, :, cols]
            wi = wv[1, x, :, cols]
            for side, (cr, ci) in enumerate(coef):
                real = cr * wr - ci * wi
                imag = cr * wi + ci * wr
                at = 2 * side * count + k * nx + x
                sums[at] = jnp.sum(real.reshape(n // 8, 8, lanes), axis=0)
                sums[at + count] = jnp.sum(imag.reshape(n // 8, 8, lanes), axis=0)
    ps[0, 0 : 4 * count, :] = jnp.sum(sums[...], axis=1)
    for load in loads:
        load.wait()


def join_kernel(*refs):
    *parts, _, out = refs
    for at, part in enumerate(parts):
        out[at] = part[0]


def route(listed, owners, place, tail):
    me = lax.axis_index("gy")
    groups, count = owners.shape
    rows = place.shape[1] // groups
    ny = place.shape[2] // 2
    ids = listed[pl.ds(me, 1), :]
    own = owners[pl.ds(me, 1), :]
    slot = slot_of(own, me, groups)
    hot = (lax.broadcasted_iota(jnp.int32, (groups, count), 0) == own).astype(f32)
    upper = (
        lax.broadcasted_iota(jnp.int32, (count, count), 0)
        < lax.broadcasted_iota(jnp.int32, (count, count), 1)
    ).astype(f32).astype(bf16)
    earlier = mm(hot.astype(bf16), upper)
    rank = jnp.sum(hot * earlier, axis=0, keepdims=True).astype(jnp.int32)
    at = lax.broadcasted_iota(jnp.int32, (groups * rows, count), 0)
    n = lax.broadcasted_iota(jnp.int32, (ny, count), 0)
    for side in range(place.shape[0]):
        total = jnp.zeros((groups * rows, ny), f32)
        for b in range(BY):
            row = rank * BY + b
            if tail is not None and side:
                row = row + jnp.where(row >= tail, 4, 0)
            here = (at == slot * rows + row).astype(f32).astype(bf16)
            there = (n == ids * BY + b).astype(f32).astype(bf16)
            total = total + mm(here, there, NT)
        place[side, :, 0:ny] = total.astype(bf16)
        place[side, :, ny : 2 * ny] = total.astype(bf16)


def solve_rows_kernel(w, y, th, tl, yh, yl):
    nx, n, wz = w.shape[1:]
    yr = y[0]
    yi = y[1]
    for part, value in ((0, (yr, -yi)), (1, (yi, yr))):
        for half in range(2):
            hi, lo = split(value[half])
            yh[part * n : (part + 1) * n, half * n : (half + 1) * n] = hi
            yl[part * n : (part + 1) * n, half * n : (half + 1) * n] = lo
    for x in range(nx):
        wx = split(w[:, x].reshape(2 * n, wz))
        hi, lo = split(mm3((yh[...], yl[...]), wx))
        rows = slice(x * n, (x + 1) * n)
        th[rows, 0:wz] = hi[0:n]
        th[rows, wz : 2 * wz] = hi[n : 2 * n]
        tl[rows, 0:wz] = lo[0:n]
        tl[rows, wz : 2 * wz] = lo[n : 2 * n]


def prepare_kernel(link, zv, iv, ov, after, edge, zsp, zed, zh, zl, place, *, tail):
    wz = zv.shape[1]
    zr = zv[0]
    zi = zv[1]
    rt = zr.T
    it = zi.T
    put(zh, zl, slice(0, wz), slice(0, wz), rt)
    put(zh, zl, slice(0, wz), slice(wz, 2 * wz), it)
    put(zh, zl, slice(wz, 2 * wz), slice(0, wz), -it)
    put(zh, zl, slice(wz, 2 * wz), slice(wz, 2 * wz), rt)
    for at, (row, turned) in enumerate(((0, False), (0, True), (wz - 1, False), (wz - 1, True))):
        edge[at : at + 1, 0:wz] = (zi if turned else zr)[row : row + 1]
        edge[at : at + 1, wz : 2 * wz] = zr[row : row + 1] if turned else -zi[row : row + 1]
    edge[4:8, :] = jnp.zeros((4, 2 * wz), f32)
    left, right = spikes_of((rt, it), link, 1)
    for at, spike in enumerate((left, right)):
        zsp[2 * at : 2 * at + 1, 0:wz] = spike[0]
        zsp[2 * at : 2 * at + 1, wz : 2 * wz] = spike[1]
        zsp[2 * at + 1 : 2 * at + 2, 0:wz] = -spike[1]
        zsp[2 * at + 1 : 2 * at + 2, wz : 2 * wz] = spike[0]
    zsp[4:8, :] = jnp.zeros((4, 2 * wz), f32)
    for at, row in enumerate(edge_rows(left, right, zed.shape[1])):
        zed[at : at + 1, :] = row
    route(iv, ov, place, tail)


def solve_columns_kernel(th, tl, zh, zl, s, base):
    n = base.shape[1]
    nx = base.shape[0] // 4
    wz = s.shape[1] // 2
    block = MBLOCK * n
    for m in range(nx // MBLOCK):
        rows = slice(m * block, (m + 1) * block)
        s[rows, :] = mm3((th[rows, :], tl[rows, :]), (zh[...], zl[...]))
    lane = lax.broadcasted_iota(jnp.int32, (n, 128), 1)
    picked = jnp.zeros((n, 128), f32)
    for at, column in enumerate((0, wz, wz - 1, 2 * wz - 1)):
        for x in range(nx):
            value = s[x * n : (x + 1) * n, column : column + 1]
            picked = jnp.where(lane == at * nx + x, value, picked)
    base[...] = picked.T[0 : 4 * nx]


def chain(gathered, nx, own, keep, index=lambda j: j):
    groups = gathered.shape[0]
    lanes = gathered.shape[2]
    zero = jnp.zeros((nx, lanes), f32)

    def read(j):
        block = gathered[index(j)]
        rows = [block[at * nx : (at + 1) * nx] for at in range(4)]
        edges = [
            jnp.broadcast_to(block[4 * nx + at : 4 * nx + at + 1], (nx, lanes))
            for at in range(EDGE)
        ]
        head, tail = (rows[0], rows[1]), (rows[2], rows[3])
        return head, tail, [(edges[2 * at], edges[2 * at + 1]) for at in range(4)]

    def forward(j, carry):
        coupling, carried = (carry[0], carry[1]), (carry[2], carry[3])
        head, tail, (lead_left, tail_left, lead_right, tail_right) = read(j)
        product = cmul(lead_left, coupling)
        pivot = (1.0 - product[0], -product[1])
        gain = cdiv(tail_left, pivot)
        for at, value in enumerate(coupling + carried + pivot):
            keep[j, at * nx : (at + 1) * nx, :] = value
        coupling_next = cadd(tail_right, cmul(gain, cmul(lead_right, coupling)))
        carried_next = cadd(
            cmul(gain, carried), cadd(tail, cmul(cmul(gain, coupling), head))
        )
        return coupling_next + carried_next

    def solved(j, head_next):
        head, _, (lead_left, _, lead_right, _) = read(j)
        kept = keep[j]
        values = [kept[at * nx : (at + 1) * nx] for at in range(6)]
        coupling, carried, pivot = (
            (values[0], values[1]),
            (values[2], values[3]),
            (values[4], values[5]),
        )
        offset = cdiv(cadd(head, cmul(lead_left, carried)), pivot)
        factor = cdiv(lead_right, pivot)
        value = cadd(offset, cmul(factor, head_next))
        return value, cadd(carried, cmul(coupling, value))

    lax.fori_loop(0, groups, forward, (zero, zero, zero, zero))
    following = lax.fori_loop(
        0,
        groups - 1 - own,
        lambda lap, head_next: solved(groups - 1 - lap, head_next)[0],
        (zero, zero),
    )
    return solved(own, following)[1], following


def row_chain_kernel(*refs):
    *parts, base, edge, zed, spk, lam, pay, keep, gathered = refs
    nx = base.shape[0] // 4
    own = lax.axis_index("gy")
    bits = len(parts) > 1
    for b, part in enumerate(parts):
        for a in range(part.shape[0]):
            gathered[a * len(parts) + b] = part[a]
    count = (gathered.shape[1] - EDGE) // 4
    sides = chain(gathered, count, own, keep, (lambda j: j ^ own) if bits else (lambda j: j))
    stacked = jnp.concatenate(
        [
            jnp.concatenate(
                [part[k : k + nx] for part in side for k in range(0, count, nx)], 1
            )
            for side in sides
        ],
        0,
    )
    lam[...] = stacked
    spikes = ((spk[0:1, :], spk[1:2, :]), (spk[2:3, :], spk[3:4, :]))
    for at in range(2):
        value = [base[(2 * at + part) * nx : (2 * at + part + 1) * nx, :] for part in range(2)]
        moved = [
            jnp.sum(stacked * edge[2 * at + part : 2 * at + part + 1, :], axis=1, keepdims=True)
            for part in range(2)
        ]
        for side in range(2):
            rows = slice(side * nx, (side + 1) * nx)
            value = cadd(value, cmul((moved[0][rows], moved[1][rows]), spikes[side]))
        pay[2 * at * nx : (2 * at + 1) * nx, :] = value[0]
        pay[(2 * at + 1) * nx : (2 * at + 2) * nx, :] = value[1]
    pay[4 * nx : 4 * nx + EDGE, :] = zed[...]


def table_kernel(listed, owners, table, phase, *rest, tail, norm):
    yt, ylast, vol, q, rank, mine = rest
    me = lax.axis_index("gy")
    groups, count = owners.shape
    rows = q.shape[0] // groups
    ny = table.shape[2]
    mine[...] = (owners[...] == me).astype(f32)
    upper = (
        lax.broadcasted_iota(jnp.int32, (count, count), 0)
        < lax.broadcasted_iota(jnp.int32, (count, count), 1)
    ).astype(f32).astype(bf16)
    rank[...] = mm(mine[...].astype(bf16), upper).astype(jnp.int32)
    at = lax.broadcasted_iota(jnp.int32, (rows, count), 0)
    n = lax.broadcasted_iota(jnp.int32, (ny, count), 0)
    order = steps_of(groups)
    for side in range(yt.shape[0]):
        for place, step in enumerate([0] + order):
            g = source_of(step, me, groups)
            own = jnp.broadcast_to(mine[pl.ds(g, 1), :], at.shape)
            total = jnp.zeros((rows, ny), f32)
            for b in range(BY):
                row = rank[pl.ds(g, 1), :] * BY + b
                if tail is not None and side:
                    row = row + jnp.where(row >= tail, 4, 0)
                here = jnp.where(at == row, own, 0.0)
                there = (n == listed[pl.ds(g, 1), :] * BY + b).astype(f32).astype(bf16)
                total = total + mm(here.astype(bf16), there, NT)
            q[place * rows : (place + 1) * rows, :] = total
        cut = (groups - late_of(groups)) * rows
        first = q[0:cut, :].astype(bf16)
        last = q[cut : groups * rows, :].astype(bf16)
        for part in range(2):
            yt[side, part] = mm(table[part], first, NT).astype(bf16)
        hi = mm(table[0], last, NT)
        lo = mm(table[1], last, NT)
        ylast[side] = jnp.concatenate([hi, hi, lo], 1).astype(bf16)
    vol[0] = jnp.cos(phase[...]) * norm
    vol[1] = jnp.sin(phase[...]) * norm


def ready_kernel(lam, zh, zl, zsp, absorber, bm, kept, moved):
    nx = lam.shape[0] // 2
    wz = lam.shape[1] // 2
    moved[...] = mm3(split(lam[...]), (zh[...], zl[...]))
    swapped = jnp.concatenate([-moved[:, wz : 2 * wz], moved[:, 0:wz]], 1)
    for x in range(nx):
        b = jnp.concatenate(
            [
                moved[x : x + 1, :],
                swapped[x : x + 1],
                moved[nx + x : nx + x + 1, :],
                swapped[nx + x : nx + x + 1],
                zsp[0:4, :],
            ],
            0,
        )
        bhi = b.astype(bf16).astype(f32)
        bm[x] = jnp.concatenate([bhi, b - bhi, bhi, jnp.zeros_like(b)], 0).astype(bf16)
        kept[x] = jnp.exp(-absorber[x])


def lost_kernel(s, spk, keep_part, bm, place, *rest, columns, groups, tail):
    parts = rest[:columns]
    am, keep, gathered = rest[-3:]
    sent = rest[columns : columns + groups]
    more = rest[columns + groups : -3]
    final = steps_of(groups)[-1]
    nx, n, wz = keep_part.shape
    own = lax.axis_index("gz")
    bits = paired_by_bits(columns)
    for step, part in enumerate(parts):
        gathered[step] = part[...]

    def index(j):
        return j ^ own if bits else (own - j + columns) % columns

    left, right = chain(gathered, nx, own, keep, index)
    for x in range(nx):
        a = jnp.concatenate(
            [spk[0:4, :]] + [v[x : x + 1] for v in (left[0], left[1], right[0], right[1])], 0
        )
        ahi = a.astype(bf16).astype(f32)
        am[x] = jnp.concatenate([ahi, ahi, a - ahi, jnp.zeros_like(a)], 0).astype(bf16)
    rows = place.shape[1] // groups
    sides = 1 if tail is None else 2
    width = rows if tail is None else 2 * tail + 8
    for step in range(nx // sides):
        parts = []
        for side in range(sides):
            x = step * sides + side
            field = s[x * n : (x + 1) * n, :] + mm(am[x], bm[x], TN)
            kept = keep_part[x]
            folded = []
            for part in range(2):
                value = field[:, part * wz : (part + 1) * wz]
                value = value - value * kept
                folded.append(sum(value[:, k * KZ : (k + 1) * KZ] for k in range(wz // KZ)))
            hi, lo = split(jnp.concatenate(folded, 1))
            parts.append(mm(place[side], jnp.concatenate([hi, lo], 0)))
        for g in range(groups):
            top = g * rows
            at = step * width
            target = sent[g]
            if g == final and at >= target.shape[0]:
                at = at - target.shape[0]
                target = more[0]
            if tail is None:
                target[at : at + rows, :] = parts[0][top : top + rows]
            else:
                target[at : at + tail, :] = parts[0][top : top + tail]
                target[at + tail : at + 2 * tail, :] = parts[1][top : top + tail]
                target[at + 2 * tail : at + 2 * tail + 8, :] = (
                    parts[0][top + tail : top + rows] + parts[1][top + tail : top + rows]
                )


def damp_kernel(s, keep_part, am, bm, damped, dv, sems):
    nx, n, wz = keep_part.shape
    copies = []
    for x in range(nx):
        field = s[x * n : (x + 1) * n, :] + mm(am[x], bm[x], TN)
        kept = keep_part[x]
        for part in range(2):
            dv[x, part] = field[:, part * wz : (part + 1) * wz] * kept
            copies.append(
                pltpu.make_async_copy(dv.at[x, part], damped.at[part, x], sems.at[x, part])
            )
            copies[-1].start()
    for copy in copies:
        copy.wait()


def plane_rows(block, x, rows, tail):
    if tail is None:
        return block[x * rows : (x + 1) * rows, :]
    at = x // 2 * (2 * tail + 8)
    side = x % 2
    return jnp.concatenate(
        [
            block[at + side * tail : at + (side + 1) * tail, :],
            block[at + 2 * tail : at + 2 * tail + 8, :],
        ],
        0,
    )


def combine(u):
    half = u.shape[0] // 2
    real = u[0:half, 0:KZ] - u[half:, KZ:]
    imag = u[0:half, KZ:] + u[half:, 0:KZ]
    return real, imag


def early_kernel(yt, ez, *rest, tail):
    count = len(rest) - 2
    got, (out, moved) = rest[:count], rest[count:]
    rows = yt.shape[3] // count
    sides = 1 if tail is None else 2
    for g in range(count):
        moved[g] = mm3(split(got[g][...]), (ez[0], ez[1]))
    for x in range(out.shape[0]):
        block = jnp.concatenate([plane_rows(moved[g], x, rows, tail) for g in range(count)], 0)
        side = x % sides
        real, imag = combine(mm3((yt[side, 0], yt[side, 1]), split(block)))
        out[x, :, 0:KZ] = real
        out[x, :, KZ:] = imag


def late_kernel(ylast, ez, early, vol, *rest, tail, first):
    out, moved, ov, sems = rest[-4:]
    sources = moved.shape[0]
    height = moved.shape[1]
    count = ov.shape[0]
    rows = ylast.shape[2] // (3 * sources)
    sides = 1 if tail is None else 2
    top = first * height // count
    for at in range(sources):
        got = rest[at]
        block = got[...] if at == sources - 1 else got[top : top + height, :]
        moved[at] = mm3(split(block), (ez[0], ez[1]))
    copies = []
    for x in range(count):
        block = [plane_rows(moved[at], x, rows, tail) for at in range(sources)]
        hi, lo = split(jnp.concatenate(block, 0))
        real, imag = combine(mm(ylast[x % sides], jnp.concatenate([hi, lo, hi], 0)))
        real = real + early[first + x, :, 0:KZ]
        imag = imag + early[first + x, :, KZ:]
        ov[x, 0] = vol[0] * real - vol[1] * imag
        ov[x, 1] = vol[0] * imag + vol[1] * real
        for part in range(2):
            copies.append(
                pltpu.make_async_copy(ov.at[x, part], out.at[part, first + x], sems.at[x, part])
            )
            copies[-1].start()
    for copy in copies:
        copy.wait()


def late_of(groups):
    return min(2, groups - 1)


def steps_of(groups):
    return list(range(1, groups))


def halves(table):
    exact = np.asarray(table, np.float64)
    hi = exact.astype(jnp.bfloat16)
    lo = (exact - hi.astype(np.float64)).astype(jnp.bfloat16)
    return np.stack([hi, lo])


def transform_tables():
    n = np.arange(KY)
    angle = 2.0 * np.pi / KY * (np.outer(n, n) % KY) - np.pi * (n % 2)[None, :]
    ytab = halves(np.concatenate([np.cos(angle), -np.sin(angle)], 0))
    n = np.arange(KZ)
    angle = 2.0 * np.pi / KZ * (np.outer(n, n) % KZ) - np.pi * (n % 2)[:, None]
    er, ei = np.cos(angle), -np.sin(angle)
    ztab = halves(np.block([[er, ei], [-ei, er]]))
    return ytab, ztab


def sds(*shape, dtype=f32):
    return jax.ShapeDtypeStruct(shape, dtype)


def body(
    wavefunction,
    absorber,
    row_inverse,
    column_inverse,
    link_terms,
    shell_blocks,
    owner_map,
    volkov_phase,
):
    nx, wy, wz = wavefunction.shape[1:]
    groups = lax.axis_size("gy")
    columns = lax.axis_size("gz")
    shell = shell_blocks.shape[2]
    capacity = 2 * ((shell + groups - 1) // groups)
    sent = capacity * BY
    paired = sent % 8 == 4 and nx % 2 == 0
    tail = sent - 4 if paired else None
    rows = (sent + 7) // 8 * 8
    sides = 2 if paired else 1
    per_plane = sent if paired else rows
    listed = shell_blocks[0]
    owners = owner_map[0, :, :, 0]
    ytab, ztab = transform_tables()
    norm = 1.0 / math.sqrt(wy * wz)

    tall = 4 * (wz // 128) * nx + EDGE
    pay, spk, wv, yv, zv, iv, ov = pl.pallas_call(
        row_edges_kernel,
        in_specs=[SM] + [AN] * 5,
        out_specs=[VM] * 7,
        out_shape=[
            sds(1, tall, 128),
            sds(8, wy),
            sds(2, nx, wy, wz),
            sds(2, wy, wy),
            sds(2, wz, wz),
            sds(*listed.shape, dtype=jnp.int32),
            sds(*owners.shape, dtype=jnp.int32),
        ],
        scratch_shapes=[
            pltpu.VMEM((tall - EDGE, 8, 128), f32),
            pltpu.SemaphoreType.DMA((nx,)),
            pltpu.SemaphoreType.DMA,
            pltpu.SemaphoreType.DMA((3,)),
        ],
        compiler_params=LIMIT,
        name="row_edges",
    )(*far(link_terms, wavefunction, row_inverse, column_inverse, listed, owners))

    inner = inner_of(groups) if paired_by_bits(groups) else groups
    outer = groups // inner
    if paired_by_bits(groups):
        lines = [pay]
        for step in range(1, outer):
            lines.append(exchange(pay, step * inner, groups))
    else:
        lines = [lax.all_gather(pay[0], "gy")]

    th, tl = pl.pallas_call(
        solve_rows_kernel,
        in_specs=[VM] * 2,
        out_specs=[VM] * 2,
        out_shape=[sds(nx * wy, 2 * wz, dtype=bf16)] * 2,
        scratch_shapes=[pltpu.VMEM((2 * wy, 2 * wy), bf16)] * 2,
        compiler_params=LIMIT,
        name="solve_rows",
    )(wv, yv)

    first = lines[-1]
    if paired_by_bits(groups):
        joined = pl.pallas_call(
            join_kernel,
            in_specs=[VM] * outer + [AN],
            out_specs=VM,
            out_shape=sds(outer, tall, 128),
            compiler_params=LIMIT,
            name="join",
        )(*lines, th)
        gathered = [joined] + [exchange(joined, step, groups) for step in range(1, inner)]
    else:
        gathered = lines

    edge, zsp, zed, zh, zl, place = pl.pallas_call(
        lambda *refs: prepare_kernel(*refs, tail=tail),
        in_specs=[SM, VM, VM, VM, AN],
        out_specs=[VM] * 6,
        out_shape=[
            sds(8, 2 * wz),
            sds(8, 2 * wz),
            sds(EDGE, wy),
            sds(2 * wz, 2 * wz, dtype=bf16),
            sds(2 * wz, 2 * wz, dtype=bf16),
            sds(sides, groups * rows, 2 * wy, dtype=bf16),
        ],
        compiler_params=LIMIT,
        name="prepare",
    )(*far(link_terms), zv, iv, ov, first)

    s, base = pl.pallas_call(
        solve_columns_kernel,
        in_specs=[VM] * 4,
        out_specs=[VM] * 2,
        out_shape=[sds(nx * wy, 2 * wz), sds(4 * nx, wy)],
        compiler_params=LIMIT,
        name="solve_columns",
    )(th, tl, zh, zl)

    lam, payz = pl.pallas_call(
        row_chain_kernel,
        in_specs=[VM] * (4 + len(gathered)),
        out_specs=[VM] * 2,
        out_shape=[sds(2 * nx, 2 * wz), sds(4 * nx + EDGE, wy)],
        scratch_shapes=[
            pltpu.VMEM((groups, 6 * (wz // 128) * nx, 128), f32),
            pltpu.VMEM((groups, tall, 128), f32),
        ],
        compiler_params=LIMIT,
        name="row_chain",
    )(*gathered, base, edge, zed, spk)

    edges = [payz]
    for step in range(1, columns):
        edges.append(exchange(payz, step, columns, "gz"))

    bm, kept = pl.pallas_call(
        ready_kernel,
        in_specs=[VM] * 5,
        out_specs=[VM] * 2,
        out_shape=[sds(nx, 32, 2 * wz, dtype=bf16), sds(nx, wy, wz)],
        scratch_shapes=[pltpu.VMEM((2 * nx, 2 * wz), f32)],
        compiler_params=LIMIT,
        name="ready",
    )(lam, zh, zl, zsp, absorber)

    height = nx * per_plane
    order = steps_of(groups)
    cuts = 2 if nx // sides % 2 == 0 else 1
    *sent, am = pl.pallas_call(
        lambda *refs: lost_kernel(*refs, columns=columns, groups=groups, tail=tail),
        in_specs=[VM] * (5 + columns),
        out_specs=[VM] * (groups + cuts),
        out_shape=[sds(height // (cuts if g == order[-1] else 1), 2 * KZ) for g in range(groups)]
        + [sds(height // cuts, 2 * KZ)] * (cuts - 1)
        + [sds(nx, 32, wy, dtype=bf16)],
        scratch_shapes=[
            pltpu.VMEM((columns, 6 * nx, wy), f32),
            pltpu.VMEM((columns, 4 * nx + EDGE, wy), f32),
        ],
        compiler_params=LIMIT,
        name="lost",
    )(s, spk, kept, bm, place, *edges)

    late = late_of(groups)
    got = [sent[0]] + [exchange(sent[step], step, groups) for step in order[:-1]]
    lasts = [exchange(part, order[-1], groups) for part in [sent[order[-1]]] + sent[groups:]]

    yt, ylast, vol = pl.pallas_call(
        lambda *refs: table_kernel(*refs, tail=tail, norm=norm),
        in_specs=[VM] * 4,
        out_specs=[VM] * 3,
        out_shape=[
            sds(sides, 2, 2 * KY, (groups - late) * rows, dtype=bf16),
            sds(sides, 2 * KY, 3 * late * rows, dtype=bf16),
            sds(2, KY, KZ),
        ],
        scratch_shapes=[
            pltpu.VMEM((groups * rows, KY), f32),
            pltpu.VMEM(owners.shape, jnp.int32),
            pltpu.VMEM(owners.shape, f32),
        ],
        compiler_params=LIMIT,
        name="tables",
    )(listed, owners, jnp.asarray(ytab), volkov_phase)

    damped = pl.pallas_call(
        damp_kernel,
        in_specs=[VM] * 4,
        out_specs=AN,
        out_shape=sds(2, nx, wy, wz),
        scratch_shapes=[
            pltpu.VMEM((nx, 2, wy, wz), f32),
            pltpu.SemaphoreType.DMA((nx, 2)),
        ],
        compiler_params=LIMIT,
        name="damp",
    )(s, kept, am, bm)

    early = pl.pallas_call(
        lambda *refs: early_kernel(*refs, tail=tail),
        in_specs=[VM] * (groups - late + 2),
        out_specs=VM,
        out_shape=sds(nx, KY, 2 * KZ),
        scratch_shapes=[pltpu.VMEM((groups - late, height, 2 * KZ), f32)],
        compiler_params=LIMIT,
        name="early",
    )(yt, jnp.asarray(ztab), *got[: groups - late])

    spectrum = []
    first = 0
    for block in lasts:
        count = block.shape[0] // per_plane
        spectrum = [
            pl.pallas_call(
                lambda *refs, first=first: late_kernel(*refs, tail=tail, first=first),
                in_specs=[VM] * (4 + late) + [AN] * len(spectrum),
                out_specs=AN,
                out_shape=sds(2, nx, KY, KZ),
                scratch_shapes=[
                    pltpu.VMEM((late, *block.shape), f32),
                    pltpu.VMEM((count, 2, KY, KZ), f32),
                    pltpu.SemaphoreType.DMA((count, 2)),
                ],
                input_output_aliases={4 + late: 0} if spectrum else {},
                compiler_params=LIMIT,
                name="late",
            )(ylast, jnp.asarray(ztab), early, vol, *got[groups - late :], block, *far(*spectrum))
        ]
        first = first + count
    (spectrum,) = spectrum
    return damped, spectrum


def solution(mesh):
    placed = (
        P(None, None, "gy", "gz"),
        P(None, "gy", "gz"),
        P(None, "gy", None),
        P(),
        P(),
        P("gz", None, None),
        P("gz", None, None, None),
        P(),
    )
    return jax.shard_map(
        body,
        mesh=mesh,
        in_specs=placed,
        out_specs=(P(None, None, "gy", "gz"), P(None, "gy", "gz", None)),
        check_vma=False,
    )
```

profile of v0, /device:TPU:8, one launch (start us, length us, event | category | flops | bytes accessed | tf_op | source)
XLA Modules:
  0.0 68.7 jit_solution(8354409079881881752)
XLA Ops:
  0.6 3.3 %row_edges.1 = (f32[1,72,128]{2,1,0:T(8,128)S(1)}, f32[8,128]{1,0:T(8,128)S(1)}, f32[2,8,128,256]{3,2,1,0:T(8,128)S(1)}, f32[2,128,128]{2,1,0:T(8,128)S(1)}, f32...) custom-call(f32[2,2,2]{2,1,0:T(2,128)} %refs_0_.1, f32[2,8,128,256]{3,2,1,0:T(8,128)} %w.1, ...), custom_call_target="tpu_custom_call" | custom-call | tf_op jit(solution)/shard_map/row_edges/pallas_call | solution.py:608
  4.0 1.6 %collective-permute-start = (f32[1,72,128]{2,1,0:T(8,128)S(1)}, f32[1,72,128]{2,1,0:T(8,128)S(1)}, u32[]{:S(2)}, u32[]{:S(2)}) collective-permute-start(f32[1,72,128]{2,1,0:T(8,128)S(1)} %get-tuple-element.43.refs_0_), channel_id=1, source_target_pairs={{0,24},{4,28},{8,16},{12,20},{16,8},{20,12},{24,0},{28,4},{1,25},{... | collective-permute-start | bytes 110600 | tf_op jit(solution)/shard_map/ppermute | solution.py:105
  5.6 2.5 %collective-permute-start.1 = (f32[1,72,128]{2,1,0:T(8,128)S(1)}, f32[1,72,128]{2,1,0:T(8,128)S(1)}, u32[]{:S(2)}, u32[]{:S(2)}) collective-permute-start(f32[1,72,128]{2,1,0:T(8,128)S(1)} %get-tuple-element.43.refs_0_), channel_id=1, source_target_pairs={{0,8},{4,12},{8,0},{12,4},{16,24},{20,28},{24,16},{28,20},{1,9},{5... | collective-permute-start | bytes 110600 | tf_op jit(solution)/shard_map/ppermute | solution.py:105
  8.1 0.0 collective-permute-start.2
  8.1 1.0 %solve_rows.1 = (bf16[1024,512]{1,0:T(8,128)(2,1)S(1)}, bf16[1024,512]{1,0:T(8,128)(2,1)S(1)}) custom-call(f32[2,8,128,256]{3,2,1,0:T(8,128)S(1)} %get-tuple-element.36.w, f32[2,128,128]{2,1,0:T(8,128)S(1)} %get-tuple-element.37.y), custom_call_target="tpu_custom_call" | custom-call | tf_op jit(solution)/shard_map/solve_rows/pallas_call | solution.py:640
  9.1 0.0 collective-permute-done.refs_4_.refs_3_
  9.1 1.3 %collective-permute-done.1.refs_1_ = f32[1,72,128]{2,1,0:T(8,128)S(1)} collective-permute-done((f32[1,72,128]{2,1,0:T(8,128)S(1)}, f32[1,72,128]{2,1,0:T(8,128)S(1)}, u32[]{:S(2)}, u32[]{:S(2)}) %collective-permute-start.1) | collective-permute-done | bytes 36896 | tf_op jit(solution)/shard_map/ppermute | solution.py:105
  10.5 2.5 %collective-permute-done.2.refs_2_ = f32[1,72,128]{2,1,0:T(8,128)S(1)} collective-permute-done((f32[1,72,128]{2,1,0:T(8,128)S(1)}, f32[1,72,128]{2,1,0:T(8,128)S(1)}, u32[]{:S(2)}, u32[]{:S(2)}) %collective-permute-start.2) | collective-permute-done | bytes 36896 | tf_op jit(solution)/shard_map/ppermute | solution.py:105
  12.9 0.0 copy-start.1
  13.0 1.6 %collective-permute-start.3 = (f32[4,72,128]{2,1,0:T(8,128)S(1)}, f32[4,72,128]{2,1,0:T(8,128)S(1)}, u32[]{:S(2)}, u32[]{:S(2)}) collective-permute-start(f32[4,72,128]{2,1,0:T(8,128)S(1)} %join.1.refs_0_), channel_id=1, source_target_pairs={{0,4},{4,0},{8,12},{12,8},{16,20},{20,16},{24,28},{28,24},{1,5},{5... | collective-permute-start | bytes 442376 | tf_op jit(solution)/shard_map/ppermute | solution.py:105
  14.5 1.1 %prepare.1 = (f32[8,512]{1,0:T(8,128)S(1)}, f32[8,512]{1,0:T(8,128)S(1)}, f32[8,128]{1,0:T(8,128)S(1)}, bf16[512,512]{1,0:T(8,128)(2,1)S(1)}, bf16[512,512]{1,0:...) custom-call(f32[2,2,2]{2,1,0:T(2,128)} %refs_0_.1, f32[2,256,256]{2,1,0:T(8,128)S(1)} %get-tuple-element.40.refs_1_, ...), custom_call_target="tpu_custom_call" | custom-call | tf_op jit(solution)/shard_map/prepare/pallas_call | solution.py:664
  15.6 2.1 %solve_columns.1 = (f32[1024,512]{1,0:T(8,128)S(1)}, f32[32,128]{1,0:T(8,128)S(1)}) custom-call(bf16[1024,512]{1,0:T(8,128)(2,1)S(1)} %get-tuple-element.38.th.refs_4_, bf16[1024,512]{1,0:T(8,128)(2,1)S(1)} %get-tuple-element.39.tl, bf16[512,512]{1,0:T(8,128)(2,1)S(1)} %get-tuple-element.44.zh, bf16[512,512]{1,0:T(8,128)(2,1)S(1)} %get-tuple-element.45.zl), custom_call_target="tpu_custom_call" | custom-call | tf_op jit(solution)/shard_map/solve_columns/pallas_call | solution.py:680
  17.7 0.4 collective-permute-done.3.refs_1_
  18.2 0.4 row_chain.1
  18.5 0.1 collective-permute-start.4
  18.6 1.6 %collective-permute-start.5 = (f32[40,128]{1,0:T(8,128)S(1)}, f32[40,128]{1,0:T(8,128)S(1)}, u32[]{:S(2)}, u32[]{:S(2)}) collective-permute-start(f32[40,128]{1,0:T(8,128)S(1)} %get-tuple-element.56.refs_5_), channel_id=1, source_target_pairs={{0,2},{1,3},{2,0},{3,1},{4,6},{5,7},{6,4},{7,5},{8,10},{9,11},{10,... | collective-permute-start | bytes 61448 | tf_op jit(solution)/shard_map/ppermute | solution.py:105
  20.2 0.3 collective-permute-start.6
  20.5 0.0 copy-done.1
  20.5 0.5 ready.1
  20.9 0.0 copy-start.2
  21.0 0.0 copy-start.3
  21.0 0.0 copy-start.4
  21.0 0.0 copy-start.5
  21.0 0.0 collective-permute-done.4.refs_6_
  21.0 1.5 %collective-permute-done.5.refs_7_ = f32[40,128]{1,0:T(8,128)S(1)} collective-permute-done((f32[40,128]{1,0:T(8,128)S(1)}, f32[40,128]{1,0:T(8,128)S(1)}, u32[]{:S(2)}, u32[]{:S(2)}) %collective-permute-start.5) | collective-permute-done | bytes 20512 | tf_op jit(solution)/shard_map/ppermute | solution.py:105
  22.5 0.9 %collective-permute-done.6.refs_8_ = f32[40,128]{1,0:T(8,128)S(1)} collective-permute-done((f32[40,128]{1,0:T(8,128)S(1)}, f32[40,128]{1,0:T(8,128)S(1)}, u32[]{:S(2)}, u32[]{:S(2)}) %collective-permute-start.6) | collective-permute-done | bytes 20512 | tf_op jit(solution)/shard_map/ppermute | solution.py:105
  23.4 1.3 %lost.1 = (f32[224,256]{1,0:T(8,128)S(1)}, f32[224,256]{1,0:T(8,128)S(1)}, f32[224,256]{1,0:T(8,128)S(1)}, f32[224,256]{1,0:T(8,128)S(1)}, f32[224,256]{1,0:T(8,...) custom-call(f32[1024,512]{1,0:T(8,128)S(1)} %get-tuple-element.46.re, ...), custom_call_target="tpu_custom_call" | custom-call | tf_op jit(solution)/shard_map/lost/pallas_call | solution.py:719
  24.6 0.4 collective-permute-start.10
  25.0 3.5 %collective-permute-start.11 = (f32[224,256]{1,0:T(8,128)S(1)}, f32[224,256]{1,0:T(8,128)S(1)}, u32[]{:S(2)}, u32[]{:S(2)}) collective-permute-start(f32[224,256]{1,0:T(8,128)S(1)} %get-tuple-element.65), channel_id=1, source_target_pairs={{0,20},{4,16},{8,28},{12,24},{16,4},{20,0},{24,12},{28,8},{1,21},{... | collective-permute-start | bytes 688136 | tf_op jit(solution)/shard_map/ppermute | solution.py:105
  28.6 0.5 collective-permute-start.7
  29.1 0.2 collective-permute-start.8
  29.3 2.8 %collective-permute-start.9 = (f32[224,256]{1,0:T(8,128)S(1)}, f32[224,256]{1,0:T(8,128)S(1)}, u32[]{:S(2)}, u32[]{:S(2)}) collective-permute-start(f32[224,256]{1,0:T(8,128)S(1)} %get-tuple-element.63), channel_id=1, source_target_pairs={{0,12},{4,8},{8,4},{12,0},{16,28},{20,24},{24,20},{28,16},{1,13},{... | collective-permute-start | bytes 688136 | tf_op jit(solution)/shard_map/ppermute | solution.py:105
  32.1 8.0 %collective-permute-done.10.refs_6_ = f32[224,256]{1,0:T(8,128)S(1)} collective-permute-done((f32[224,256]{1,0:T(8,128)S(1)}, f32[224,256]{1,0:T(8,128)S(1)}, u32[]{:S(2)}, u32[]{:S(2)}) %collective-permute-start.10) | collective-permute-done | bytes 229408 | tf_op jit(solution)/shard_map/ppermute | solution.py:105
  40.1 2.2 %collective-permute-start.12 = (f32[224,256]{1,0:T(8,128)S(1)}, f32[224,256]{1,0:T(8,128)S(1)}, u32[]{:S(2)}, u32[]{:S(2)}) collective-permute-start(f32[224,256]{1,0:T(8,128)S(1)} %get-tuple-element.67), channel_id=1, source_target_pairs={{0,24},{4,28},{8,16},{12,20},{16,8},{20,12},{24,0},{28,4},{1,25},{... | collective-permute-start | bytes 688136 | tf_op jit(solution)/shard_map/ppermute | solution.py:105
  42.2 3.0 %collective-permute-done.11.refs_7_ = f32[224,256]{1,0:T(8,128)S(1)} collective-permute-done((f32[224,256]{1,0:T(8,128)S(1)}, f32[224,256]{1,0:T(8,128)S(1)}, u32[]{:S(2)}, u32[]{:S(2)}) %collective-permute-start.11) | collective-permute-done | bytes 229408 | tf_op jit(solution)/shard_map/ppermute | solution.py:105
  45.3 2.7 %collective-permute-start.14 = (f32[112,256]{1,0:T(8,128)S(1)}, f32[112,256]{1,0:T(8,128)S(1)}, u32[]{:S(2)}, u32[]{:S(2)}) collective-permute-start(f32[112,256]{1,0:T(8,128)S(1)} %get-tuple-element.69), channel_id=1, source_target_pairs={{0,28},{4,24},{8,20},{12,16},{16,12},{20,8},{24,4},{28,0},{1,29},{... | collective-permute-start | bytes 344072 | tf_op jit(solution)/shard_map/ppermute | solution.py:105
  48.0 0.0 collective-permute-done.7.refs_3_
  48.0 0.2 collective-permute-start.13
  48.2 0.0 copy-done.2
  48.2 0.0 copy-done.3
  48.2 0.0 copy-done.4
  48.2 0.0 copy-done.5
  48.2 1.6 %tables.1 = (bf16[2,2,256,192]{3,2,1,0:T(8,128)(2,1)S(1)}, bf16[2,256,192]{2,1,0:T(8,128)(2,1)S(1)}, f32[2,128,128]{2,1,0:T(8,128)S(1)}) custom-call(s32[8,56]{1,0:T(8,128)S(1)} %bitcast.3, s32[8,56]{1,0:T(8,128)S(1)} %bitcast.5, bf16[2,256,128]{2,1,0:T(8,128)(2,1)S(1)} %copy-done.2, f32[128,128]{1,0:T(8,128)S(1)} %copy-done.3), custom_call_target="tpu_custom_call" | custom-call | tf_op jit(solution)/shard_map/tables/pallas_call | solution.py:738
  49.8 0.0 copy-start
  49.8 1.7 %damp.1 = f32[2,8,128,256]{3,2,1,0:T(8,128)} custom-call(f32[1024,512]{1,0:T(8,128)S(1)} %get-tuple-element.46.refs_0_.s, f32[8,128,256]{2,1,0:T(8,128)S(1)} %get-tuple-element.53.refs_2_.keep_part, bf16[8,32,128]{2,1,0:T(8,128)(2,1)S(1)} %get-tuple-element.57.am, bf16[8,32,512]{2,1,0:T(8,128)(2,1)S(1)} %get-tuple-element.54.refs_3_.bm), custom_call_target="tpu_custom_call" | custom-call | tf_op jit(solution)/shard_map/damp/pallas_call | solution.py:756
  51.4 0.0 collective-permute-done.8.refs_4_
  51.5 0.0 collective-permute-done.9.refs_5_
  51.5 0.0 copy-done
  51.5 1.7 %early.1.refs_2_ = f32[8,128,256]{2,1,0:T(8,128)S(1)} custom-call(bf16[2,2,256,192]{3,2,1,0:T(8,128)(2,1)S(1)} %get-tuple-element.59.refs_0_, bf16[2,256,256]{2,1,0:T(8,128)(2,1)S(1)} %copy-done, f32[224,256]{1,0:T(8,128)S(1)} %get-tuple-element.60.refs_2_, f32[224,256]{1,0:T(8,128)S(1)} %collective-permute-done.7.refs_3_, ...), custom_call_target="tpu_custom_call" | custom-call | tf_op jit(solution)/shard_map/early/pallas_call | solution.py:769
  53.1 12.6 %collective-permute-done.14.refs_5_ = f32[112,256]{1,0:T(8,128)S(1)} collective-permute-done((f32[112,256]{1,0:T(8,128)S(1)}, f32[112,256]{1,0:T(8,128)S(1)}, u32[]{:S(2)}, u32[]{:S(2)}) %collective-permute-start.14) | collective-permute-done | bytes 114720 | tf_op jit(solution)/shard_map/ppermute | solution.py:105
  65.8 0.0 collective-permute-done.12.refs_4_
  65.8 1.3 %late.2.refs_6_ = f32[2,8,128,128]{3,2,1,0:T(8,128)} custom-call(bf16[2,256,192]{2,1,0:T(8,128)(2,1)S(1)} %get-tuple-element.58.refs_0_, bf16[2,256,256]{2,1,0:T(8,128)(2,1)S(1)} %copy-done, f32[8,128,256]{2,1,0:T(8,128)S(1)} %early.1.refs_2_, f32[2,128,128]{2,1,0:T(8,128)S(1)} %get-tuple-element.66.refs_3_, f32[224,256]{1,0:T(8,128)S(1)} %collective-permute-done.12.refs_4_, ...), custom_call_target="tpu_custom_call" | custom-call | tf_op jit(solution)/shard_map/late/pallas_call | solution.py:784
  67.1 0.3 collective-permute-done.13.refs_5_
  67.4 1.3 %late.3 = f32[2,8,128,128]{3,2,1,0:T(8,128)} custom-call(bf16[2,256,192]{2,1,0:T(8,128)(2,1)S(1)} %get-tuple-element.58.refs_0_, bf16[2,256,256]{2,1,0:T(8,128)(2,1)S(1)} %copy-done, f32[8,128,256]{2,1,0:T(8,128)S(1)} %early.1.refs_2_, f32[2,128,128]{2,1,0:T(8,128)S(1)} %get-tuple-element.66.refs_3_, ...), custom_call_target="tpu_custom_call", output_to_operand_aliasing={{}: (6, {})} | custom-call | tf_op jit(solution)/shard_map/late/pallas_call | solution.py:784
  (1 shorter events, 0.0 us)
Async XLA Ops:
  4.0 5.1 %collective-permute-start = (f32[1,72,128]{2,1,0:T(8,128)S(1)}, f32[1,72,128]{2,1,0:T(8,128)S(1)}, u32[]{:S(2)}, u32[]{:S(2)}) collective-permute-start(f32[1,72,128]{2,1,0:T(8,128)S(1)} %get-tuple-element.43.refs_0_), channel_id=1, source_target_pairs={{0,24},{4,28},{8,16},{12,20},{16,8},{20,12},{24,0},{28,4},{1,25},{... | collective-permute-start | bytes 110600 | tf_op jit(solution)/shard_map/ppermute | solution.py:105
  5.6 4.9 %collective-permute-start.1 = (f32[1,72,128]{2,1,0:T(8,128)S(1)}, f32[1,72,128]{2,1,0:T(8,128)S(1)}, u32[]{:S(2)}, u32[]{:S(2)}) collective-permute-start(f32[1,72,128]{2,1,0:T(8,128)S(1)} %get-tuple-element.43.refs_0_), channel_id=1, source_target_pairs={{0,8},{4,12},{8,0},{12,4},{16,24},{20,28},{24,16},{28,20},{1,9},{5... | collective-permute-start | bytes 110600 | tf_op jit(solution)/shard_map/ppermute | solution.py:105
  8.1 4.9 %collective-permute-start.2 = (f32[1,72,128]{2,1,0:T(8,128)S(1)}, f32[1,72,128]{2,1,0:T(8,128)S(1)}, u32[]{:S(2)}, u32[]{:S(2)}) collective-permute-start(f32[1,72,128]{2,1,0:T(8,128)S(1)} %get-tuple-element.43.refs_0_), channel_id=1, source_target_pairs={{0,16},{4,20},{8,24},{12,28},{16,0},{20,4},{24,8},{28,12},{1,17},{... | collective-permute-start | bytes 110600 | tf_op jit(solution)/shard_map/ppermute | solution.py:105
  12.9 7.5 %copy-start.1 = (f32[8,128,256]{2,1,0:T(8,128)S(1)}, f32[8,128,256]{2,1,0:T(8,128)}, u32[]{:S(2)}) copy-start(f32[8,128,256]{2,1,0:T(8,128)} %absorber.1) | copy-start | bytes 3145732
  13.0 5.2 %collective-permute-start.3 = (f32[4,72,128]{2,1,0:T(8,128)S(1)}, f32[4,72,128]{2,1,0:T(8,128)S(1)}, u32[]{:S(2)}, u32[]{:S(2)}) collective-permute-start(f32[4,72,128]{2,1,0:T(8,128)S(1)} %join.1.refs_0_), channel_id=1, source_target_pairs={{0,4},{4,0},{8,12},{12,8},{16,20},{20,16},{24,28},{28,24},{1,5},{5... | collective-permute-start | bytes 442376 | tf_op jit(solution)/shard_map/ppermute | solution.py:105
  18.5 2.4 %collective-permute-start.4 = (f32[40,128]{1,0:T(8,128)S(1)}, f32[40,128]{1,0:T(8,128)S(1)}, u32[]{:S(2)}, u32[]{:S(2)}) collective-permute-start(f32[40,128]{1,0:T(8,128)S(1)} %get-tuple-element.56.refs_5_), channel_id=1, source_target_pairs={{0,1},{1,0},{2,3},{3,2},{4,5},{5,4},{6,7},{7,6},{8,9},{9,8},{10,11... | collective-permute-start | bytes 61448 | tf_op jit(solution)/shard_map/ppermute | solution.py:105
  18.6 3.8 %collective-permute-start.5 = (f32[40,128]{1,0:T(8,128)S(1)}, f32[40,128]{1,0:T(8,128)S(1)}, u32[]{:S(2)}, u32[]{:S(2)}) collective-permute-start(f32[40,128]{1,0:T(8,128)S(1)} %get-tuple-element.56.refs_5_), channel_id=1, source_target_pairs={{0,2},{1,3},{2,0},{3,1},{4,6},{5,7},{6,4},{7,5},{8,10},{9,11},{10,... | collective-permute-start | bytes 61448 | tf_op jit(solution)/shard_map/ppermute | solution.py:105
  20.2 3.2 %collective-permute-start.6 = (f32[40,128]{1,0:T(8,128)S(1)}, f32[40,128]{1,0:T(8,128)S(1)}, u32[]{:S(2)}, u32[]{:S(2)}) collective-permute-start(f32[40,128]{1,0:T(8,128)S(1)} %get-tuple-element.56.refs_5_), channel_id=1, source_target_pairs={{0,3},{1,2},{2,1},{3,0},{4,7},{5,6},{6,5},{7,4},{8,11},{9,10},{10,... | collective-permute-start | bytes 61448 | tf_op jit(solution)/shard_map/ppermute | solution.py:105
  20.9 27.2 %copy-start.2 = (bf16[2,256,128]{2,1,0:T(8,128)(2,1)S(1)}, bf16[2,256,128]{2,1,0:T(8,128)(2,1)}, u32[]{:S(2)}) copy-start(bf16[2,256,128]{2,1,0:T(8,128)(2,1)} %constant.4.clone.refs_2_) | copy-start | bytes 393220
  21.0 27.2 %copy-start.3 = (f32[128,128]{1,0:T(8,128)S(1)}, f32[128,128]{1,0:T(8,128)}, u32[]{:S(2)}) copy-start(f32[128,128]{1,0:T(8,128)} %refs_3_.1) | copy-start | bytes 196612
  21.0 27.2 %copy-start.4 = (s32[1,8,56]{2,1,0:T(8,128)S(1)}, s32[1,8,56]{2,1,0:T(8,128)}, u32[]{:S(2)}) copy-start(s32[1,8,56]{2,1,0:T(8,128)} %param.15) | copy-start | bytes 5380
  21.0 27.2 %copy-start.5 = (s32[1,8,56,1]{2,3,1,0:T(1,128)S(1)}, s32[1,8,56,1]{2,3,1,0:T(1,128)}, u32[]{:S(2)}) copy-start(s32[1,8,56,1]{2,3,1,0:T(1,128)} %param.16) | copy-start | bytes 5380
  24.6 15.4 %collective-permute-start.10 = (f32[224,256]{1,0:T(8,128)S(1)}, f32[224,256]{1,0:T(8,128)S(1)}, u32[]{:S(2)}, u32[]{:S(2)}) collective-permute-start(f32[224,256]{1,0:T(8,128)S(1)} %get-tuple-element.64), channel_id=1, source_target_pairs={{0,16},{4,20},{8,24},{12,28},{16,0},{20,4},{24,8},{28,12},{1,17},{... | collective-permute-start | bytes 688136 | tf_op jit(solution)/shard_map/ppermute | solution.py:105
  25.0 20.2 %collective-permute-start.11 = (f32[224,256]{1,0:T(8,128)S(1)}, f32[224,256]{1,0:T(8,128)S(1)}, u32[]{:S(2)}, u32[]{:S(2)}) collective-permute-start(f32[224,256]{1,0:T(8,128)S(1)} %get-tuple-element.65), channel_id=1, source_target_pairs={{0,20},{4,16},{8,28},{12,24},{16,4},{20,0},{24,12},{28,8},{1,21},{... | collective-permute-start | bytes 688136 | tf_op jit(solution)/shard_map/ppermute | solution.py:105
  28.6 19.4 %collective-permute-start.7 = (f32[224,256]{1,0:T(8,128)S(1)}, f32[224,256]{1,0:T(8,128)S(1)}, u32[]{:S(2)}, u32[]{:S(2)}) collective-permute-start(f32[224,256]{1,0:T(8,128)S(1)} %get-tuple-element.61), channel_id=1, source_target_pairs={{0,4},{4,0},{8,12},{12,8},{16,20},{20,16},{24,28},{28,24},{1,5},{5... | collective-permute-start | bytes 688136 | tf_op jit(solution)/shard_map/ppermute | solution.py:105
  29.1 22.3 %collective-permute-start.8 = (f32[224,256]{1,0:T(8,128)S(1)}, f32[224,256]{1,0:T(8,128)S(1)}, u32[]{:S(2)}, u32[]{:S(2)}) collective-permute-start(f32[224,256]{1,0:T(8,128)S(1)} %get-tuple-element.62), channel_id=1, source_target_pairs={{0,8},{4,12},{8,0},{12,4},{16,24},{20,28},{24,16},{28,20},{1,9},{5... | collective-permute-start | bytes 688136 | tf_op jit(solution)/shard_map/ppermute | solution.py:105
  29.3 22.2 %collective-permute-start.9 = (f32[224,256]{1,0:T(8,128)S(1)}, f32[224,256]{1,0:T(8,128)S(1)}, u32[]{:S(2)}, u32[]{:S(2)}) collective-permute-start(f32[224,256]{1,0:T(8,128)S(1)} %get-tuple-element.63), channel_id=1, source_target_pairs={{0,12},{4,8},{8,4},{12,0},{16,28},{20,24},{24,20},{28,16},{1,13},{... | collective-permute-start | bytes 688136 | tf_op jit(solution)/shard_map/ppermute | solution.py:105
  40.1 25.7 %collective-permute-start.12 = (f32[224,256]{1,0:T(8,128)S(1)}, f32[224,256]{1,0:T(8,128)S(1)}, u32[]{:S(2)}, u32[]{:S(2)}) collective-permute-start(f32[224,256]{1,0:T(8,128)S(1)} %get-tuple-element.67), channel_id=1, source_target_pairs={{0,24},{4,28},{8,16},{12,20},{16,8},{20,12},{24,0},{28,4},{1,25},{... | collective-permute-start | bytes 688136 | tf_op jit(solution)/shard_map/ppermute | solution.py:105
  45.3 20.5 %collective-permute-start.14 = (f32[112,256]{1,0:T(8,128)S(1)}, f32[112,256]{1,0:T(8,128)S(1)}, u32[]{:S(2)}, u32[]{:S(2)}) collective-permute-start(f32[112,256]{1,0:T(8,128)S(1)} %get-tuple-element.69), channel_id=1, source_target_pairs={{0,28},{4,24},{8,20},{12,16},{16,12},{20,8},{24,4},{28,0},{1,29},{... | collective-permute-start | bytes 344072 | tf_op jit(solution)/shard_map/ppermute | solution.py:105
  48.0 19.4 %collective-permute-start.13 = (f32[112,256]{1,0:T(8,128)S(1)}, f32[112,256]{1,0:T(8,128)S(1)}, u32[]{:S(2)}, u32[]{:S(2)}) collective-permute-start(f32[112,256]{1,0:T(8,128)S(1)} %get-tuple-element.68), channel_id=1, source_target_pairs={{0,28},{4,24},{8,20},{12,16},{16,12},{20,8},{24,4},{28,0},{1,29},{... | collective-permute-start | bytes 344072 | tf_op jit(solution)/shard_map/ppermute | solution.py:105
  49.8 1.7 %copy-start = (bf16[2,256,256]{2,1,0:T(8,128)(2,1)S(1)}, bf16[2,256,256]{2,1,0:T(8,128)(2,1)}, u32[]{:S(2)}) copy-start(bf16[2,256,256]{2,1,0:T(8,128)(2,1)} %constant.5.clone.refs_1_) | copy-start | bytes 786436
where the time goes:
time: 68.9 us; the launch traced here: 68.7 us
  waiting for transfers between devices  30.6 us (44%)
  starting transfers between devices  20.1 us (29%)
  Pallas kernels  17.2 us (25%)
  between operations  0.81 us (1%)
    ppermute x15, waiting for transfers between devices, exchange(): return lax.ppermute(value, axis, pairs)  30.6 us
    ppermute x15, starting transfers between devices, exchange(): return lax.ppermute(value, axis, pairs)  20.1 us
    pallas_call x1, Pallas kernels, body(): pl.pallas_call(row_edges_kernel, in_specs=[SM] + [AN] * 5, out_specs=[VM]...  3.32 us
    pallas_call x2, Pallas kernels, body(): pl.pallas_call(lambda *refs, first=first: late_kernel(*refs, tail=tail, f...  2.68 us
    pallas_call x1, Pallas kernels, body(): pl.pallas_call(solve_columns_kernel, in_specs=[VM] * 4, out_specs=[VM] *...  2.12 us
    pallas_call x1, Pallas kernels, body(): pl.pallas_call(damp_kernel, in_specs=[VM] * 4, out_specs=AN, out_shape=sd...  1.66 us
    pallas_call x1, Pallas kernels, body(): pl.pallas_call(lambda *refs: early_kernel(*refs, tail=tail), in_specs=[VM...  1.65 us
    pallas_call x1, Pallas kernels, body(): pl.pallas_call(lambda *refs: table_kernel(*refs, tail=tail, norm=norm), i...  1.56 us
  transfers between devices with their start and end apart: 15, of which 9 were waited for; matrix products, arithmetic and copies ran while one was open for 0% of the time, Pallas kernels for 16%

commit v1 on v0

--- a/solution.py
+++ b/solution.py
@@ -111,11 +111,13 @@
 
 
 def row_edges_kernel(
-    link, w, y, col, listed, owners, ps, spk, wv, yv, zv, iv, ov, sums, sems, ysem, zsems
+    terms, w, y, col, listed, owners, ps, spk, wv, yv, zv, iv, ov, link, sums, sems, ysem, zsems, lsem
 ):
     nx, n, width = wv.shape[1:]
     ycopy = pltpu.make_async_copy(y, yv, ysem)
     ycopy.start()
+    linked = pltpu.make_async_copy(terms, link, lsem)
+    linked.start()
     copies = []
     for x in range(nx):
         copies.append(pltpu.make_async_copy(w.at[:, x], wv.at[:, x], sems.at[x]))
@@ -130,6 +132,7 @@
     for load in loads:
         load.start()
     ycopy.wait()
+    linked.wait()
     rt = yv[0].T
     it = yv[1].T
     left, right = spikes_of((rt, it), link, 0)
@@ -607,7 +610,7 @@
     tall = 4 * (wz // 128) * nx + EDGE
     pay, spk, wv, yv, zv, iv, ov = pl.pallas_call(
         row_edges_kernel,
-        in_specs=[SM] + [AN] * 5,
+        in_specs=[AN] * 6,
         out_specs=[VM] * 7,
         out_shape=[
             sds(1, tall, 128),
@@ -619,10 +622,12 @@
             sds(*owners.shape, dtype=jnp.int32),
         ],
         scratch_shapes=[
+            pltpu.SMEM(link_terms.shape, f32),
             pltpu.VMEM((tall - EDGE, 8, 128), f32),
             pltpu.SemaphoreType.DMA((nx,)),
             pltpu.SemaphoreType.DMA,
             pltpu.SemaphoreType.DMA((3,)),
+            pltpu.SemaphoreType.DMA,
         ],
         compiler_params=LIMIT,
         name="row_edges",

time: 68.9 us -> 68.2 us (0.990)
  Pallas kernels: 17.2 us -> 16.5 us
where the time goes in v1:
time: 68.2 us; the launch traced here: 68 us
  waiting for transfers between devices  30.6 us (45%)
  starting transfers between devices  20.1 us (29%)
  Pallas kernels  16.5 us (24%)
  between operations  0.81 us (1%)
    ppermute x15, waiting for transfers between devices, exchange(): return lax.ppermute(value, axis, pairs)  30.6 us
    ppermute x15, starting transfers between devices, exchange(): return lax.ppermute(value, axis, pairs)  20.1 us
    pallas_call x2, Pallas kernels, body(): pl.pallas_call(lambda *refs, first=first: late_kernel(*refs, tail=tail, f...  2.68 us
    pallas_call x1, Pallas kernels, body(): pl.pallas_call(row_edges_kernel, in_specs=[AN] * 6, out_specs=[VM] * 7, o...  2.65 us
    pallas_call x1, Pallas kernels, body(): pl.pallas_call(solve_columns_kernel, in_specs=[VM] * 4, out_specs=[VM] *...  2.12 us
    pallas_call x1, Pallas kernels, body(): pl.pallas_call(damp_kernel, in_specs=[VM] * 4, out_specs=AN, out_shape=sd...  1.66 us
    pallas_call x1, Pallas kernels, body(): pl.pallas_call(lambda *refs: early_kernel(*refs, tail=tail), in_specs=[VM...  1.65 us
    pallas_call x1, Pallas kernels, body(): pl.pallas_call(lambda *refs: table_kernel(*refs, tail=tail, norm=norm), i...  1.56 us
  transfers between devices with their start and end apart: 15, of which 9 were waited for; matrix products, arithmetic and copies ran while one was open for 0% of the time, Pallas kernels for 16%

profile of v1, /device:TPU:8, one launch (start us, length us, event | category | flops | bytes accessed | tf_op | source)
XLA Modules:
  0.0 68.0 jit_solution(7194276492590178591)
XLA Ops:
  0.6 2.6 %row_edges.1 = (f32[1,72,128]{2,1,0:T(8,128)S(1)}, f32[8,128]{1,0:T(8,128)S(1)}, f32[2,8,128,256]{3,2,1,0:T(8,128)S(1)}, f32[2,128,128]{2,1,0:T(8,128)S(1)}, f32...) custom-call(f32[2,2,2]{2,1,0:T(2,128)} %refs_0_.1, f32[2,8,128,256]{3,2,1,0:T(8,128)} %w.1, ...), custom_call_target="tpu_custom_call" | custom-call | tf_op jit(solution)/shard_map/row_edges/pallas_call | solution.py:611
  3.3 1.6 %collective-permute-start = (f32[1,72,128]{2,1,0:T(8,128)S(1)}, f32[1,72,128]{2,1,0:T(8,128)S(1)}, u32[]{:S(2)}, u32[]{:S(2)}) collective-permute-start(f32[1,72,128]{2,1,0:T(8,128)S(1)} %get-tuple-element.43.refs_0_), channel_id=1, source_target_pairs={{0,24},{4,28},{8,16},{12,20},{16,8},{20,12},{24,0},{28,4},{1,25},{... | collective-permute-start | bytes 110600 | tf_op jit(solution)/shard_map/ppermute | solution.py:105
  4.9 2.5 %collective-permute-start.1 = (f32[1,72,128]{2,1,0:T(8,128)S(1)}, f32[1,72,128]{2,1,0:T(8,128)S(1)}, u32[]{:S(2)}, u32[]{:S(2)}) collective-permute-start(f32[1,72,128]{2,1,0:T(8,128)S(1)} %get-tuple-element.43.refs_0_), channel_id=1, source_target_pairs={{0,8},{4,12},{8,0},{12,4},{16,24},{20,28},{24,16},{28,20},{1,9},{5... | collective-permute-start | bytes 110600 | tf_op jit(solution)/shard_map/ppermute | solution.py:105
  7.4 0.0 collective-permute-start.2
  7.4 1.0 %solve_rows.1 = (bf16[1024,512]{1,0:T(8,128)(2,1)S(1)}, bf16[1024,512]{1,0:T(8,128)(2,1)S(1)}) custom-call(f32[2,8,128,256]{3,2,1,0:T(8,128)S(1)} %get-tuple-element.36.w, f32[2,128,128]{2,1,0:T(8,128)S(1)} %get-tuple-element.37.y), custom_call_target="tpu_custom_call" | custom-call | tf_op jit(solution)/shard_map/solve_rows/pallas_call | solution.py:645
  8.4 0.0 collective-permute-done.refs_4_.refs_3_
  8.4 1.3 %collective-permute-done.1.refs_1_ = f32[1,72,128]{2,1,0:T(8,128)S(1)} collective-permute-done((f32[1,72,128]{2,1,0:T(8,128)S(1)}, f32[1,72,128]{2,1,0:T(8,128)S(1)}, u32[]{:S(2)}, u32[]{:S(2)}) %collective-permute-start.1) | collective-permute-done | bytes 36896 | tf_op jit(solution)/shard_map/ppermute | solution.py:105
  9.8 2.5 %collective-permute-done.2.refs_2_ = f32[1,72,128]{2,1,0:T(8,128)S(1)} collective-permute-done((f32[1,72,128]{2,1,0:T(8,128)S(1)}, f32[1,72,128]{2,1,0:T(8,128)S(1)}, u32[]{:S(2)}, u32[]{:S(2)}) %collective-permute-start.2) | collective-permute-done | bytes 36896 | tf_op jit(solution)/shard_map/ppermute | solution.py:105
  12.3 0.0 copy-start.1
  12.3 1.6 %collective-permute-start.3 = (f32[4,72,128]{2,1,0:T(8,128)S(1)}, f32[4,72,128]{2,1,0:T(8,128)S(1)}, u32[]{:S(2)}, u32[]{:S(2)}) collective-permute-start(f32[4,72,128]{2,1,0:T(8,128)S(1)} %join.1.refs_0_), channel_id=1, source_target_pairs={{0,4},{4,0},{8,12},{12,8},{16,20},{20,16},{24,28},{28,24},{1,5},{5... | collective-permute-start | bytes 442376 | tf_op jit(solution)/shard_map/ppermute | solution.py:105
  13.9 1.1 %prepare.1 = (f32[8,512]{1,0:T(8,128)S(1)}, f32[8,512]{1,0:T(8,128)S(1)}, f32[8,128]{1,0:T(8,128)S(1)}, bf16[512,512]{1,0:T(8,128)(2,1)S(1)}, bf16[512,512]{1,0:...) custom-call(f32[2,2,2]{2,1,0:T(2,128)} %refs_0_.1, f32[2,256,256]{2,1,0:T(8,128)S(1)} %get-tuple-element.40.refs_1_, ...), custom_call_target="tpu_custom_call" | custom-call | tf_op jit(solution)/shard_map/prepare/pallas_call | solution.py:669
  15.0 2.1 %solve_columns.1 = (f32[1024,512]{1,0:T(8,128)S(1)}, f32[32,128]{1,0:T(8,128)S(1)}) custom-call(bf16[1024,512]{1,0:T(8,128)(2,1)S(1)} %get-tuple-element.38.th.refs_4_, bf16[1024,512]{1,0:T(8,128)(2,1)S(1)} %get-tuple-element.39.tl, bf16[512,512]{1,0:T(8,128)(2,1)S(1)} %get-tuple-element.44.zh, bf16[512,512]{1,0:T(8,128)(2,1)S(1)} %get-tuple-element.45.zl), custom_call_target="tpu_custom_call" | custom-call | tf_op jit(solution)/shard_map/solve_columns/pallas_call | solution.py:685
  17.1 0.4 collective-permute-done.3.refs_1_
  17.5 0.4 row_chain.1
  17.9 0.1 collective-permute-start.4
  17.9 1.6 %collective-permute-start.5 = (f32[40,128]{1,0:T(8,128)S(1)}, f32[40,128]{1,0:T(8,128)S(1)}, u32[]{:S(2)}, u32[]{:S(2)}) collective-permute-start(f32[40,128]{1,0:T(8,128)S(1)} %get-tuple-element.56.refs_5_), channel_id=1, source_target_pairs={{0,2},{1,3},{2,0},{3,1},{4,6},{5,7},{6,4},{7,5},{8,10},{9,11},{10,... | collective-permute-start | bytes 61448 | tf_op jit(solution)/shard_map/ppermute | solution.py:105
  19.5 0.3 collective-permute-start.6
  19.8 0.0 copy-done.1
  19.8 0.5 ready.1
  20.3 0.0 copy-start.2
  20.3 0.0 copy-start.3
  20.3 0.0 copy-start.4
  20.3 0.0 copy-start.5
  20.3 0.0 collective-permute-done.4.refs_6_
  20.3 1.5 %collective-permute-done.5.refs_7_ = f32[40,128]{1,0:T(8,128)S(1)} collective-permute-done((f32[40,128]{1,0:T(8,128)S(1)}, f32[40,128]{1,0:T(8,128)S(1)}, u32[]{:S(2)}, u32[]{:S(2)}) %collective-permute-start.5) | collective-permute-done | bytes 20512 | tf_op jit(solution)/shard_map/ppermute | solution.py:105
  21.8 0.9 %collective-permute-done.6.refs_8_ = f32[40,128]{1,0:T(8,128)S(1)} collective-permute-done((f32[40,128]{1,0:T(8,128)S(1)}, f32[40,128]{1,0:T(8,128)S(1)}, u32[]{:S(2)}, u32[]{:S(2)}) %collective-permute-start.6) | collective-permute-done | bytes 20512 | tf_op jit(solution)/shard_map/ppermute | solution.py:105
  22.7 1.3 %lost.1 = (f32[224,256]{1,0:T(8,128)S(1)}, f32[224,256]{1,0:T(8,128)S(1)}, f32[224,256]{1,0:T(8,128)S(1)}, f32[224,256]{1,0:T(8,128)S(1)}, f32[224,256]{1,0:T(8,...) custom-call(f32[1024,512]{1,0:T(8,128)S(1)} %get-tuple-element.46.re, ...), custom_call_target="tpu_custom_call" | custom-call | tf_op jit(solution)/shard_map/lost/pallas_call | solution.py:724
  24.0 0.4 collective-permute-start.10
  24.4 3.5 %collective-permute-start.11 = (f32[224,256]{1,0:T(8,128)S(1)}, f32[224,256]{1,0:T(8,128)S(1)}, u32[]{:S(2)}, u32[]{:S(2)}) collective-permute-start(f32[224,256]{1,0:T(8,128)S(1)} %get-tuple-element.65), channel_id=1, source_target_pairs={{0,20},{4,16},{8,28},{12,24},{16,4},{20,0},{24,12},{28,8},{1,21},{... | collective-permute-start | bytes 688136 | tf_op jit(solution)/shard_map/ppermute | solution.py:105
  27.9 0.5 collective-permute-start.7
  28.4 0.2 collective-permute-start.8
  28.6 2.8 %collective-permute-start.9 = (f32[224,256]{1,0:T(8,128)S(1)}, f32[224,256]{1,0:T(8,128)S(1)}, u32[]{:S(2)}, u32[]{:S(2)}) collective-permute-start(f32[224,256]{1,0:T(8,128)S(1)} %get-tuple-element.63), channel_id=1, source_target_pairs={{0,12},{4,8},{8,4},{12,0},{16,28},{20,24},{24,20},{28,16},{1,13},{... | collective-permute-start | bytes 688136 | tf_op jit(solution)/shard_map/ppermute | solution.py:105
  31.4 8.0 %collective-permute-done.10.refs_6_ = f32[224,256]{1,0:T(8,128)S(1)} collective-permute-done((f32[224,256]{1,0:T(8,128)S(1)}, f32[224,256]{1,0:T(8,128)S(1)}, u32[]{:S(2)}, u32[]{:S(2)}) %collective-permute-start.10) | collective-permute-done | bytes 229408 | tf_op jit(solution)/shard_map/ppermute | solution.py:105
  39.4 2.2 %collective-permute-start.12 = (f32[224,256]{1,0:T(8,128)S(1)}, f32[224,256]{1,0:T(8,128)S(1)}, u32[]{:S(2)}, u32[]{:S(2)}) collective-permute-start(f32[224,256]{1,0:T(8,128)S(1)} %get-tuple-element.67), channel_id=1, source_target_pairs={{0,24},{4,28},{8,16},{12,20},{16,8},{20,12},{24,0},{28,4},{1,25},{... | collective-permute-start | bytes 688136 | tf_op jit(solution)/shard_map/ppermute | solution.py:105
  41.6 3.0 %collective-permute-done.11.refs_7_ = f32[224,256]{1,0:T(8,128)S(1)} collective-permute-done((f32[224,256]{1,0:T(8,128)S(1)}, f32[224,256]{1,0:T(8,128)S(1)}, u32[]{:S(2)}, u32[]{:S(2)}) %collective-permute-start.11) | collective-permute-done | bytes 229408 | tf_op jit(solution)/shard_map/ppermute | solution.py:105
  44.6 2.7 %collective-permute-start.14 = (f32[112,256]{1,0:T(8,128)S(1)}, f32[112,256]{1,0:T(8,128)S(1)}, u32[]{:S(2)}, u32[]{:S(2)}) collective-permute-start(f32[112,256]{1,0:T(8,128)S(1)} %get-tuple-element.69), channel_id=1, source_target_pairs={{0,28},{4,24},{8,20},{12,16},{16,12},{20,8},{24,4},{28,0},{1,29},{... | collective-permute-start | bytes 344072 | tf_op jit(solution)/shard_map/ppermute | solution.py:105
  47.3 0.0 collective-permute-done.7.refs_3_
  47.3 0.2 collective-permute-start.13
  47.5 0.0 copy-done.2
  47.5 0.0 copy-done.3
  47.5 0.0 copy-done.4
  47.5 0.0 copy-done.5
  47.5 1.6 %tables.1 = (bf16[2,2,256,192]{3,2,1,0:T(8,128)(2,1)S(1)}, bf16[2,256,192]{2,1,0:T(8,128)(2,1)S(1)}, f32[2,128,128]{2,1,0:T(8,128)S(1)}) custom-call(s32[8,56]{1,0:T(8,128)S(1)} %bitcast.3, s32[8,56]{1,0:T(8,128)S(1)} %bitcast.5, bf16[2,256,128]{2,1,0:T(8,128)(2,1)S(1)} %copy-done.2, f32[128,128]{1,0:T(8,128)S(1)} %copy-done.3), custom_call_target="tpu_custom_call" | custom-call | tf_op jit(solution)/shard_map/tables/pallas_call | solution.py:743
  49.1 0.0 copy-start
  49.1 1.7 %damp.1 = f32[2,8,128,256]{3,2,1,0:T(8,128)} custom-call(f32[1024,512]{1,0:T(8,128)S(1)} %get-tuple-element.46.refs_0_.s, f32[8,128,256]{2,1,0:T(8,128)S(1)} %get-tuple-element.53.refs_2_.keep_part, bf16[8,32,128]{2,1,0:T(8,128)(2,1)S(1)} %get-tuple-element.57.am, bf16[8,32,512]{2,1,0:T(8,128)(2,1)S(1)} %get-tuple-element.54.refs_3_.bm), custom_call_target="tpu_custom_call" | custom-call | tf_op jit(solution)/shard_map/damp/pallas_call | solution.py:761
  50.8 0.0 collective-permute-done.8.refs_4_
  50.8 0.0 collective-permute-done.9.refs_5_
  50.8 0.0 copy-done
  50.8 1.7 %early.1.refs_2_ = f32[8,128,256]{2,1,0:T(8,128)S(1)} custom-call(bf16[2,2,256,192]{3,2,1,0:T(8,128)(2,1)S(1)} %get-tuple-element.59.refs_0_, bf16[2,256,256]{2,1,0:T(8,128)(2,1)S(1)} %copy-done, f32[224,256]{1,0:T(8,128)S(1)} %get-tuple-element.60.refs_2_, f32[224,256]{1,0:T(8,128)S(1)} %collective-permute-done.7.refs_3_, ...), custom_call_target="tpu_custom_call" | custom-call | tf_op jit(solution)/shard_map/early/pallas_call | solution.py:774
  52.5 12.6 %collective-permute-done.14.refs_5_ = f32[112,256]{1,0:T(8,128)S(1)} collective-permute-done((f32[112,256]{1,0:T(8,128)S(1)}, f32[112,256]{1,0:T(8,128)S(1)}, u32[]{:S(2)}, u32[]{:S(2)}) %collective-permute-start.14) | collective-permute-done | bytes 114720 | tf_op jit(solution)/shard_map/ppermute | solution.py:105
  65.1 0.0 collective-permute-done.12.refs_4_
  65.1 1.3 %late.2.refs_6_ = f32[2,8,128,128]{3,2,1,0:T(8,128)} custom-call(bf16[2,256,192]{2,1,0:T(8,128)(2,1)S(1)} %get-tuple-element.58.refs_0_, bf16[2,256,256]{2,1,0:T(8,128)(2,1)S(1)} %copy-done, f32[8,128,256]{2,1,0:T(8,128)S(1)} %early.1.refs_2_, f32[2,128,128]{2,1,0:T(8,128)S(1)} %get-tuple-element.66.refs_3_, f32[224,256]{1,0:T(8,128)S(1)} %collective-permute-done.12.refs_4_, ...), custom_call_target="tpu_custom_call" | custom-call | tf_op jit(solution)/shard_map/late/pallas_call | solution.py:789
  66.4 0.3 collective-permute-done.13.refs_5_
  66.7 1.3 %late.3 = f32[2,8,128,128]{3,2,1,0:T(8,128)} custom-call(bf16[2,256,192]{2,1,0:T(8,128)(2,1)S(1)} %get-tuple-element.58.refs_0_, bf16[2,256,256]{2,1,0:T(8,128)(2,1)S(1)} %copy-done, f32[8,128,256]{2,1,0:T(8,128)S(1)} %early.1.refs_2_, f32[2,128,128]{2,1,0:T(8,128)S(1)} %get-tuple-element.66.refs_3_, ...), custom_call_target="tpu_custom_call", output_to_operand_aliasing={{}: (6, {})} | custom-call | tf_op jit(solution)/shard_map/late/pallas_call | solution.py:789
  (1 shorter events, 0.0 us)
Async XLA Ops:
  3.3 5.1 %collective-permute-start = (f32[1,72,128]{2,1,0:T(8,128)S(1)}, f32[1,72,128]{2,1,0:T(8,128)S(1)}, u32[]{:S(2)}, u32[]{:S(2)}) collective-permute-start(f32[1,72,128]{2,1,0:T(8,128)S(1)} %get-tuple-element.43.refs_0_), channel_id=1, source_target_pairs={{0,24},{4,28},{8,16},{12,20},{16,8},{20,12},{24,0},{28,4},{1,25},{... | collective-permute-start | bytes 110600 | tf_op jit(solution)/shard_map/ppermute | solution.py:105
  4.9 4.9 %collective-permute-start.1 = (f32[1,72,128]{2,1,0:T(8,128)S(1)}, f32[1,72,128]{2,1,0:T(8,128)S(1)}, u32[]{:S(2)}, u32[]{:S(2)}) collective-permute-start(f32[1,72,128]{2,1,0:T(8,128)S(1)} %get-tuple-element.43.refs_0_), channel_id=1, source_target_pairs={{0,8},{4,12},{8,0},{12,4},{16,24},{20,28},{24,16},{28,20},{1,9},{5... | collective-permute-start | bytes 110600 | tf_op jit(solution)/shard_map/ppermute | solution.py:105
  7.4 4.9 %collective-permute-start.2 = (f32[1,72,128]{2,1,0:T(8,128)S(1)}, f32[1,72,128]{2,1,0:T(8,128)S(1)}, u32[]{:S(2)}, u32[]{:S(2)}) collective-permute-start(f32[1,72,128]{2,1,0:T(8,128)S(1)} %get-tuple-element.43.refs_0_), channel_id=1, source_target_pairs={{0,16},{4,20},{8,24},{12,28},{16,0},{20,4},{24,8},{28,12},{1,17},{... | collective-permute-start | bytes 110600 | tf_op jit(solution)/shard_map/ppermute | solution.py:105
  12.3 7.5 %copy-start.1 = (f32[8,128,256]{2,1,0:T(8,128)S(1)}, f32[8,128,256]{2,1,0:T(8,128)}, u32[]{:S(2)}) copy-start(f32[8,128,256]{2,1,0:T(8,128)} %absorber.1) | copy-start | bytes 3145732
  12.3 5.2 %collective-permute-start.3 = (f32[4,72,128]{2,1,0:T(8,128)S(1)}, f32[4,72,128]{2,1,0:T(8,128)S(1)}, u32[]{:S(2)}, u32[]{:S(2)}) collective-permute-start(f32[4,72,128]{2,1,0:T(8,128)S(1)} %join.1.refs_0_), channel_id=1, source_target_pairs={{0,4},{4,0},{8,12},{12,8},{16,20},{20,16},{24,28},{28,24},{1,5},{5... | collective-permute-start | bytes 442376 | tf_op jit(solution)/shard_map/ppermute | solution.py:105
  17.9 2.4 %collective-permute-start.4 = (f32[40,128]{1,0:T(8,128)S(1)}, f32[40,128]{1,0:T(8,128)S(1)}, u32[]{:S(2)}, u32[]{:S(2)}) collective-permute-start(f32[40,128]{1,0:T(8,128)S(1)} %get-tuple-element.56.refs_5_), channel_id=1, source_target_pairs={{0,1},{1,0},{2,3},{3,2},{4,5},{5,4},{6,7},{7,6},{8,9},{9,8},{10,11... | collective-permute-start | bytes 61448 | tf_op jit(solution)/shard_map/ppermute | solution.py:105
  17.9 3.8 %collective-permute-start.5 = (f32[40,128]{1,0:T(8,128)S(1)}, f32[40,128]{1,0:T(8,128)S(1)}, u32[]{:S(2)}, u32[]{:S(2)}) collective-permute-start(f32[40,128]{1,0:T(8,128)S(1)} %get-tuple-element.56.refs_5_), channel_id=1, source_target_pairs={{0,2},{1,3},{2,0},{3,1},{4,6},{5,7},{6,4},{7,5},{8,10},{9,11},{10,... | collective-permute-start | bytes 61448 | tf_op jit(solution)/shard_map/ppermute | solution.py:105
  19.5 3.2 %collective-permute-start.6 = (f32[40,128]{1,0:T(8,128)S(1)}, f32[40,128]{1,0:T(8,128)S(1)}, u32[]{:S(2)}, u32[]{:S(2)}) collective-permute-start(f32[40,128]{1,0:T(8,128)S(1)} %get-tuple-element.56.refs_5_), channel_id=1, source_target_pairs={{0,3},{1,2},{2,1},{3,0},{4,7},{5,6},{6,5},{7,4},{8,11},{9,10},{10,... | collective-permute-start | bytes 61448 | tf_op jit(solution)/shard_map/ppermute | solution.py:105
  20.3 27.2 %copy-start.2 = (bf16[2,256,128]{2,1,0:T(8,128)(2,1)S(1)}, bf16[2,256,128]{2,1,0:T(8,128)(2,1)}, u32[]{:S(2)}) copy-start(bf16[2,256,128]{2,1,0:T(8,128)(2,1)} %constant.4.clone.refs_2_) | copy-start | bytes 393220
  20.3 27.2 %copy-start.3 = (f32[128,128]{1,0:T(8,128)S(1)}, f32[128,128]{1,0:T(8,128)}, u32[]{:S(2)}) copy-start(f32[128,128]{1,0:T(8,128)} %refs_3_.1) | copy-start | bytes 196612
  20.3 27.2 %copy-start.4 = (s32[1,8,56]{2,1,0:T(8,128)S(1)}, s32[1,8,56]{2,1,0:T(8,128)}, u32[]{:S(2)}) copy-start(s32[1,8,56]{2,1,0:T(8,128)} %param.15) | copy-start | bytes 5380
  20.3 27.2 %copy-start.5 = (s32[1,8,56,1]{2,3,1,0:T(1,128)S(1)}, s32[1,8,56,1]{2,3,1,0:T(1,128)}, u32[]{:S(2)}) copy-start(s32[1,8,56,1]{2,3,1,0:T(1,128)} %param.16) | copy-start | bytes 5380
  24.0 15.4 %collective-permute-start.10 = (f32[224,256]{1,0:T(8,128)S(1)}, f32[224,256]{1,0:T(8,128)S(1)}, u32[]{:S(2)}, u32[]{:S(2)}) collective-permute-start(f32[224,256]{1,0:T(8,128)S(1)} %get-tuple-element.64), channel_id=1, source_target_pairs={{0,16},{4,20},{8,24},{12,28},{16,0},{20,4},{24,8},{28,12},{1,17},{... | collective-permute-start | bytes 688136 | tf_op jit(solution)/shard_map/ppermute | solution.py:105
  24.4 20.2 %collective-permute-start.11 = (f32[224,256]{1,0:T(8,128)S(1)}, f32[224,256]{1,0:T(8,128)S(1)}, u32[]{:S(2)}, u32[]{:S(2)}) collective-permute-start(f32[224,256]{1,0:T(8,128)S(1)} %get-tuple-element.65), channel_id=1, source_target_pairs={{0,20},{4,16},{8,28},{12,24},{16,4},{20,0},{24,12},{28,8},{1,21},{... | collective-permute-start | bytes 688136 | tf_op jit(solution)/shard_map/ppermute | solution.py:105
  27.9 19.4 %collective-permute-start.7 = (f32[224,256]{1,0:T(8,128)S(1)}, f32[224,256]{1,0:T(8,128)S(1)}, u32[]{:S(2)}, u32[]{:S(2)}) collective-permute-start(f32[224,256]{1,0:T(8,128)S(1)} %get-tuple-element.61), channel_id=1, source_target_pairs={{0,4},{4,0},{8,12},{12,8},{16,20},{20,16},{24,28},{28,24},{1,5},{5... | collective-permute-start | bytes 688136 | tf_op jit(solution)/shard_map/ppermute | solution.py:105
  28.4 22.3 %collective-permute-start.8 = (f32[224,256]{1,0:T(8,128)S(1)}, f32[224,256]{1,0:T(8,128)S(1)}, u32[]{:S(2)}, u32[]{:S(2)}) collective-permute-start(f32[224,256]{1,0:T(8,128)S(1)} %get-tuple-element.62), channel_id=1, source_target_pairs={{0,8},{4,12},{8,0},{12,4},{16,24},{20,28},{24,16},{28,20},{1,9},{5... | collective-permute-start | bytes 688136 | tf_op jit(solution)/shard_map/ppermute | solution.py:105
  28.6 22.2 %collective-permute-start.9 = (f32[224,256]{1,0:T(8,128)S(1)}, f32[224,256]{1,0:T(8,128)S(1)}, u32[]{:S(2)}, u32[]{:S(2)}) collective-permute-start(f32[224,256]{1,0:T(8,128)S(1)} %get-tuple-element.63), channel_id=1, source_target_pairs={{0,12},{4,8},{8,4},{12,0},{16,28},{20,24},{24,20},{28,16},{1,13},{... | collective-permute-start | bytes 688136 | tf_op jit(solution)/shard_map/ppermute | solution.py:105
  39.4 25.7 %collective-permute-start.12 = (f32[224,256]{1,0:T(8,128)S(1)}, f32[224,256]{1,0:T(8,128)S(1)}, u32[]{:S(2)}, u32[]{:S(2)}) collective-permute-start(f32[224,256]{1,0:T(8,128)S(1)} %get-tuple-element.67), channel_id=1, source_target_pairs={{0,24},{4,28},{8,16},{12,20},{16,8},{20,12},{24,0},{28,4},{1,25},{... | collective-permute-start | bytes 688136 | tf_op jit(solution)/shard_map/ppermute | solution.py:105
  44.6 20.5 %collective-permute-start.14 = (f32[112,256]{1,0:T(8,128)S(1)}, f32[112,256]{1,0:T(8,128)S(1)}, u32[]{:S(2)}, u32[]{:S(2)}) collective-permute-start(f32[112,256]{1,0:T(8,128)S(1)} %get-tuple-element.69), channel_id=1, source_target_pairs={{0,28},{4,24},{8,20},{12,16},{16,12},{20,8},{24,4},{28,0},{1,29},{... | collective-permute-start | bytes 344072 | tf_op jit(solution)/shard_map/ppermute | solution.py:105
  47.3 19.4 %collective-permute-start.13 = (f32[112,256]{1,0:T(8,128)S(1)}, f32[112,256]{1,0:T(8,128)S(1)}, u32[]{:S(2)}, u32[]{:S(2)}) collective-permute-start(f32[112,256]{1,0:T(8,128)S(1)} %get-tuple-element.68), channel_id=1, source_target_pairs={{0,28},{4,24},{8,20},{12,16},{16,12},{20,8},{24,4},{28,0},{1,29},{... | collective-permute-start | bytes 344072 | tf_op jit(solution)/shard_map/ppermute | solution.py:105
  49.1 1.7 %copy-start = (bf16[2,256,256]{2,1,0:T(8,128)(2,1)S(1)}, bf16[2,256,256]{2,1,0:T(8,128)(2,1)}, u32[]{:S(2)}) copy-start(bf16[2,256,256]{2,1,0:T(8,128)(2,1)} %constant.5.clone.refs_1_) | copy-start | bytes 786436

commit v2 on v1

--- a/solution.py
+++ b/solution.py
@@ -54,15 +54,10 @@
     lo_ref[rows, cols] = lo
 
 
-def spikes_of(transposed, link, sweep):
+def spikes_of(transposed, previous, following):
     last = transposed[0].shape[0] - 1
-    left = cmul(
-        (link[sweep, 0, 0], link[sweep, 0, 1]), (transposed[0][0:1], transposed[1][0:1])
-    )
-    right = cmul(
-        (link[sweep, 1, 0], link[sweep, 1, 1]),
-        (transposed[0][last : last + 1], transposed[1][last : last + 1]),
-    )
+    left = cmul(previous, (transposed[0][0:1], transposed[1][0:1]))
+    right = cmul(following, (transposed[0][last : last + 1], transposed[1][last : last + 1]))
     return left, right
 
 
@@ -135,10 +130,13 @@
     linked.wait()
     rt = yv[0].T
     it = yv[1].T
-    left, right = spikes_of((rt, it), link, 0)
+    left, right = spikes_of(
+        (rt, it), (link[0, 0, 0], link[0, 0, 1]), (link[0, 1, 0], link[0, 1, 1])
+    )
     for at, row in enumerate((left[0], left[1], right[0], right[1])):
         spk[at : at + 1, :] = row
-    spk[4:8, :] = jnp.zeros((4, n), f32)
+    for at in range(4):
+        spk[4 + at : 5 + at, :] = jnp.full((1, n), link[1, at // 2, at % 2], f32)
     lanes = ps.shape[2]
     count = width // lanes * nx
     for at, row in enumerate(edge_rows(left, right, lanes)):
@@ -222,7 +220,7 @@
         tl[rows, wz : 2 * wz] = lo[n : 2 * n]
 
 
-def prepare_kernel(link, zv, iv, ov, after, edge, zsp, zed, zh, zl, place, *, tail):
+def prepare_kernel(spk, zv, iv, ov, after, edge, zsp, zed, zh, zl, place, *, tail):
     wz = zv.shape[1]
     zr = zv[0]
     zi = zv[1]
@@ -236,7 +234,8 @@
         edge[at : at + 1, 0:wz] = (zi if turned else zr)[row : row + 1]
         edge[at : at + 1, wz : 2 * wz] = zr[row : row + 1] if turned else -zi[row : row + 1]
     edge[4:8, :] = jnp.zeros((4, 2 * wz), f32)
-    left, right = spikes_of((rt, it), link, 1)
+    terms = [spk[at : at + 1, 0:1] for at in range(4, 8)]
+    left, right = spikes_of((rt, it), (terms[0], terms[1]), (terms[2], terms[3]))
     for at, spike in enumerate((left, right)):
         zsp[2 * at : 2 * at + 1, 0:wz] = spike[0]
         zsp[2 * at : 2 * at + 1, wz : 2 * wz] = spike[1]
@@ -668,7 +667,7 @@
 
     edge, zsp, zed, zh, zl, place = pl.pallas_call(
         lambda *refs: prepare_kernel(*refs, tail=tail),
-        in_specs=[SM, VM, VM, VM, AN],
+        in_specs=[VM, VM, VM, VM, AN],
         out_specs=[VM] * 6,
         out_shape=[
             sds(8, 2 * wz),
@@ -680,7 +679,7 @@
         ],
         compiler_params=LIMIT,
         name="prepare",
-    )(*far(link_terms), zv, iv, ov, first)
+    )(spk, zv, iv, ov, first)
 
     s, base = pl.pallas_call(
         solve_columns_kernel,

time: 68.2 us -> 68.2 us (level)
  Pallas kernels: 16.5 us -> 15.8 us
    ppermute x15, waiting for transfers between devices: 30.6 us -> 31.2 us  [exchange(): return lax.ppermute(value, axis, pairs)]
    pallas_call x1, Pallas kernels: 1.08 us -> 0.39 us  [body(): pl.pallas_call(lambda *refs: prepare_kernel(*refs, tail=tail), in_specs=[...]
  transfers between devices with their start and end apart: 15 -> 15, of which waited for: 9 -> 9; matrix products, arithmetic and copies ran while one was open for 0% -> 0% of each run, Pallas kernels for 16% -> 15%
where the time goes in v2:
time: 68.2 us; the launch traced here: 68 us
  waiting for transfers between devices  31.2 us (46%)
  starting transfers between devices  20.1 us (29%)
  Pallas kernels  15.8 us (23%)
  between operations  0.81 us (1%)
    ppermute x15, waiting for transfers between devices, exchange(): return lax.ppermute(value, axis, pairs)  31.2 us
    ppermute x15, starting transfers between devices, exchange(): return lax.ppermute(value, axis, pairs)  20.1 us
    pallas_call x2, Pallas kernels, body(): pl.pallas_call(lambda *refs, first=first: late_kernel(*refs, tail=tail, f...  2.68 us
    pallas_call x1, Pallas kernels, body(): pl.pallas_call(row_edges_kernel, in_specs=[AN] * 6, out_specs=[VM] * 7, o...  2.65 us
    pallas_call x1, Pallas kernels, body(): pl.pallas_call(solve_columns_kernel, in_specs=[VM] * 4, out_specs=[VM] *...  2.12 us
    pallas_call x1, Pallas kernels, body(): pl.pallas_call(damp_kernel, in_specs=[VM] * 4, out_specs=AN, out_shape=sd...  1.66 us
    pallas_call x1, Pallas kernels, body(): pl.pallas_call(lambda *refs: early_kernel(*refs, tail=tail), in_specs=[VM...  1.65 us
    pallas_call x1, Pallas kernels, body(): pl.pallas_call(lambda *refs: table_kernel(*refs, tail=tail, norm=norm), i...  1.56 us
  transfers between devices with their start and end apart: 15, of which 9 were waited for; matrix products, arithmetic and copies ran while one was open for 0% of the time, Pallas kernels for 15%

profile of v2, /device:TPU:8, one launch (start us, length us, event | category | flops | bytes accessed | tf_op | source)
XLA Modules:
  0.0 68.0 jit_solution(2757909852410938150)
XLA Ops:
  0.6 2.6 %row_edges.1 = (f32[1,72,128]{2,1,0:T(8,128)S(1)}, f32[8,128]{1,0:T(8,128)S(1)}, f32[2,8,128,256]{3,2,1,0:T(8,128)S(1)}, f32[2,128,128]{2,1,0:T(8,128)S(1)}, f32...) custom-call(f32[2,2,2]{2,1,0:T(2,128)} %terms.1, f32[2,8,128,256]{3,2,1,0:T(8,128)} %w.1, ...), custom_call_target="tpu_custom_call" | custom-call | tf_op jit(solution)/shard_map/row_edges/pallas_call | solution.py:610
  3.3 1.6 %collective-permute-start = (f32[1,72,128]{2,1,0:T(8,128)S(1)}, f32[1,72,128]{2,1,0:T(8,128)S(1)}, u32[]{:S(2)}, u32[]{:S(2)}) collective-permute-start(f32[1,72,128]{2,1,0:T(8,128)S(1)} %get-tuple-element.44.refs_0_), channel_id=1, source_target_pairs={{0,24},{4,28},{8,16},{12,20},{16,8},{20,12},{24,0},{28,4},{1,25},{... | collective-permute-start | bytes 110600 | tf_op jit(solution)/shard_map/ppermute | solution.py:100
  4.9 2.5 %collective-permute-start.1 = (f32[1,72,128]{2,1,0:T(8,128)S(1)}, f32[1,72,128]{2,1,0:T(8,128)S(1)}, u32[]{:S(2)}, u32[]{:S(2)}) collective-permute-start(f32[1,72,128]{2,1,0:T(8,128)S(1)} %get-tuple-element.44.refs_0_), channel_id=1, source_target_pairs={{0,8},{4,12},{8,0},{12,4},{16,24},{20,28},{24,16},{28,20},{1,9},{5... | collective-permute-start | bytes 110600 | tf_op jit(solution)/shard_map/ppermute | solution.py:100
  7.4 0.0 collective-permute-start.2
  7.4 1.0 %solve_rows.1 = (bf16[1024,512]{1,0:T(8,128)(2,1)S(1)}, bf16[1024,512]{1,0:T(8,128)(2,1)S(1)}) custom-call(f32[2,8,128,256]{3,2,1,0:T(8,128)S(1)} %get-tuple-element.36.w, f32[2,128,128]{2,1,0:T(8,128)S(1)} %get-tuple-element.37.y), custom_call_target="tpu_custom_call" | custom-call | tf_op jit(solution)/shard_map/solve_rows/pallas_call | solution.py:644
  8.4 0.0 collective-permute-done.refs_4_.refs_3_
  8.4 1.3 %collective-permute-done.1.refs_1_ = f32[1,72,128]{2,1,0:T(8,128)S(1)} collective-permute-done((f32[1,72,128]{2,1,0:T(8,128)S(1)}, f32[1,72,128]{2,1,0:T(8,128)S(1)}, u32[]{:S(2)}, u32[]{:S(2)}) %collective-permute-start.1) | collective-permute-done | bytes 36896 | tf_op jit(solution)/shard_map/ppermute | solution.py:100
  9.8 2.5 %collective-permute-done.2.refs_2_ = f32[1,72,128]{2,1,0:T(8,128)S(1)} collective-permute-done((f32[1,72,128]{2,1,0:T(8,128)S(1)}, f32[1,72,128]{2,1,0:T(8,128)S(1)}, u32[]{:S(2)}, u32[]{:S(2)}) %collective-permute-start.2) | collective-permute-done | bytes 36896 | tf_op jit(solution)/shard_map/ppermute | solution.py:100
  12.3 0.0 copy-start.1
  12.3 1.6 %collective-permute-start.3 = (f32[4,72,128]{2,1,0:T(8,128)S(1)}, f32[4,72,128]{2,1,0:T(8,128)S(1)}, u32[]{:S(2)}, u32[]{:S(2)}) collective-permute-start(f32[4,72,128]{2,1,0:T(8,128)S(1)} %join.1.refs_0_), channel_id=1, source_target_pairs={{0,4},{4,0},{8,12},{12,8},{16,20},{20,16},{24,28},{28,24},{1,5},{5... | collective-permute-start | bytes 442376 | tf_op jit(solution)/shard_map/ppermute | solution.py:100
  13.9 0.4 prepare.1
  14.3 2.1 %solve_columns.1 = (f32[1024,512]{1,0:T(8,128)S(1)}, f32[32,128]{1,0:T(8,128)S(1)}) custom-call(bf16[1024,512]{1,0:T(8,128)(2,1)S(1)} %get-tuple-element.38.th.refs_4_, bf16[1024,512]{1,0:T(8,128)(2,1)S(1)} %get-tuple-element.39.tl, bf16[512,512]{1,0:T(8,128)(2,1)S(1)} %get-tuple-element.45.zh, bf16[512,512]{1,0:T(8,128)(2,1)S(1)} %get-tuple-element.46.zl), custom_call_target="tpu_custom_call" | custom-call | tf_op jit(solution)/shard_map/solve_columns/pallas_call | solution.py:684
  16.4 1.1 %collective-permute-done.3.refs_1_ = f32[4,72,128]{2,1,0:T(8,128)S(1)} collective-permute-done((f32[4,72,128]{2,1,0:T(8,128)S(1)}, f32[4,72,128]{2,1,0:T(8,128)S(1)}, u32[]{:S(2)}, u32[]{:S(2)}) %collective-permute-start.3) | collective-permute-done | bytes 147488 | tf_op jit(solution)/shard_map/ppermute | solution.py:100
  17.5 0.4 row_chain.1
  17.9 0.1 collective-permute-start.4
  17.9 1.6 %collective-permute-start.5 = (f32[40,128]{1,0:T(8,128)S(1)}, f32[40,128]{1,0:T(8,128)S(1)}, u32[]{:S(2)}, u32[]{:S(2)}) collective-permute-start(f32[40,128]{1,0:T(8,128)S(1)} %get-tuple-element.56.refs_5_), channel_id=1, source_target_pairs={{0,2},{1,3},{2,0},{3,1},{4,6},{5,7},{6,4},{7,5},{8,10},{9,11},{10,... | collective-permute-start | bytes 61448 | tf_op jit(solution)/shard_map/ppermute | solution.py:100
  19.5 0.3 collective-permute-start.6
  19.8 0.0 copy-done.1
  19.8 0.5 ready.1
  20.3 0.0 copy-start.2
  20.3 0.0 copy-start.3
  20.3 0.0 copy-start.4
  20.3 0.0 copy-start.5
  20.3 0.0 collective-permute-done.4.refs_6_
  20.3 1.5 %collective-permute-done.5.refs_7_ = f32[40,128]{1,0:T(8,128)S(1)} collective-permute-done((f32[40,128]{1,0:T(8,128)S(1)}, f32[40,128]{1,0:T(8,128)S(1)}, u32[]{:S(2)}, u32[]{:S(2)}) %collective-permute-start.5) | collective-permute-done | bytes 20512 | tf_op jit(solution)/shard_map/ppermute | solution.py:100
  21.8 0.9 %collective-permute-done.6.refs_8_ = f32[40,128]{1,0:T(8,128)S(1)} collective-permute-done((f32[40,128]{1,0:T(8,128)S(1)}, f32[40,128]{1,0:T(8,128)S(1)}, u32[]{:S(2)}, u32[]{:S(2)}) %collective-permute-start.6) | collective-permute-done | bytes 20512 | tf_op jit(solution)/shard_map/ppermute | solution.py:100
  22.7 1.3 %lost.1 = (f32[224,256]{1,0:T(8,128)S(1)}, f32[224,256]{1,0:T(8,128)S(1)}, f32[224,256]{1,0:T(8,128)S(1)}, f32[224,256]{1,0:T(8,128)S(1)}, f32[224,256]{1,0:T(8,...) custom-call(f32[1024,512]{1,0:T(8,128)S(1)} %get-tuple-element.47.re, ...), custom_call_target="tpu_custom_call" | custom-call | tf_op jit(solution)/shard_map/lost/pallas_call | solution.py:723
  24.0 0.4 collective-permute-start.10
  24.4 3.5 %collective-permute-start.11 = (f32[224,256]{1,0:T(8,128)S(1)}, f32[224,256]{1,0:T(8,128)S(1)}, u32[]{:S(2)}, u32[]{:S(2)}) collective-permute-start(f32[224,256]{1,0:T(8,128)S(1)} %get-tuple-element.65), channel_id=1, source_target_pairs={{0,20},{4,16},{8,28},{12,24},{16,4},{20,0},{24,12},{28,8},{1,21},{... | collective-permute-start | bytes 688136 | tf_op jit(solution)/shard_map/ppermute | solution.py:100
  27.9 0.5 collective-permute-start.7
  28.4 0.2 collective-permute-start.8
  28.6 2.8 %collective-permute-start.9 = (f32[224,256]{1,0:T(8,128)S(1)}, f32[224,256]{1,0:T(8,128)S(1)}, u32[]{:S(2)}, u32[]{:S(2)}) collective-permute-start(f32[224,256]{1,0:T(8,128)S(1)} %get-tuple-element.63), channel_id=1, source_target_pairs={{0,12},{4,8},{8,4},{12,0},{16,28},{20,24},{24,20},{28,16},{1,13},{... | collective-permute-start | bytes 688136 | tf_op jit(solution)/shard_map/ppermute | solution.py:100
  31.4 8.0 %collective-permute-done.10.refs_6_ = f32[224,256]{1,0:T(8,128)S(1)} collective-permute-done((f32[224,256]{1,0:T(8,128)S(1)}, f32[224,256]{1,0:T(8,128)S(1)}, u32[]{:S(2)}, u32[]{:S(2)}) %collective-permute-start.10) | collective-permute-done | bytes 229408 | tf_op jit(solution)/shard_map/ppermute | solution.py:100
  39.4 2.2 %collective-permute-start.12 = (f32[224,256]{1,0:T(8,128)S(1)}, f32[224,256]{1,0:T(8,128)S(1)}, u32[]{:S(2)}, u32[]{:S(2)}) collective-permute-start(f32[224,256]{1,0:T(8,128)S(1)} %get-tuple-element.67), channel_id=1, source_target_pairs={{0,24},{4,28},{8,16},{12,20},{16,8},{20,12},{24,0},{28,4},{1,25},{... | collective-permute-start | bytes 688136 | tf_op jit(solution)/shard_map/ppermute | solution.py:100
  41.6 3.0 %collective-permute-done.11.refs_7_ = f32[224,256]{1,0:T(8,128)S(1)} collective-permute-done((f32[224,256]{1,0:T(8,128)S(1)}, f32[224,256]{1,0:T(8,128)S(1)}, u32[]{:S(2)}, u32[]{:S(2)}) %collective-permute-start.11) | collective-permute-done | bytes 229408 | tf_op jit(solution)/shard_map/ppermute | solution.py:100
  44.6 2.7 %collective-permute-start.14 = (f32[112,256]{1,0:T(8,128)S(1)}, f32[112,256]{1,0:T(8,128)S(1)}, u32[]{:S(2)}, u32[]{:S(2)}) collective-permute-start(f32[112,256]{1,0:T(8,128)S(1)} %get-tuple-element.69), channel_id=1, source_target_pairs={{0,28},{4,24},{8,20},{12,16},{16,12},{20,8},{24,4},{28,0},{1,29},{... | collective-permute-start | bytes 344072 | tf_op jit(solution)/shard_map/ppermute | solution.py:100
  47.3 0.0 collective-permute-done.7.refs_3_
  47.3 0.2 collective-permute-start.13
  47.5 0.0 copy-done.2
  47.5 0.0 copy-done.3
  47.5 0.0 copy-done.4
  47.5 0.0 copy-done.5
  47.5 1.6 %tables.1 = (bf16[2,2,256,192]{3,2,1,0:T(8,128)(2,1)S(1)}, bf16[2,256,192]{2,1,0:T(8,128)(2,1)S(1)}, f32[2,128,128]{2,1,0:T(8,128)S(1)}) custom-call(s32[8,56]{1,0:T(8,128)S(1)} %bitcast.3, s32[8,56]{1,0:T(8,128)S(1)} %bitcast.5, bf16[2,256,128]{2,1,0:T(8,128)(2,1)S(1)} %copy-done.2, f32[128,128]{1,0:T(8,128)S(1)} %copy-done.3), custom_call_target="tpu_custom_call" | custom-call | tf_op jit(solution)/shard_map/tables/pallas_call | solution.py:742
  49.1 0.0 copy-start
  49.1 1.7 %damp.1 = f32[2,8,128,256]{3,2,1,0:T(8,128)} custom-call(f32[1024,512]{1,0:T(8,128)S(1)} %get-tuple-element.47.refs_0_.s, f32[8,128,256]{2,1,0:T(8,128)S(1)} %get-tuple-element.53.refs_2_.keep_part, bf16[8,32,128]{2,1,0:T(8,128)(2,1)S(1)} %get-tuple-element.57.am, bf16[8,32,512]{2,1,0:T(8,128)(2,1)S(1)} %get-tuple-element.54.refs_3_.bm), custom_call_target="tpu_custom_call" | custom-call | tf_op jit(solution)/shard_map/damp/pallas_call | solution.py:760
  50.8 0.0 collective-permute-done.8.refs_4_
  50.8 0.0 collective-permute-done.9.refs_5_
  50.8 0.0 copy-done
  50.8 1.7 %early.1.refs_2_ = f32[8,128,256]{2,1,0:T(8,128)S(1)} custom-call(bf16[2,2,256,192]{3,2,1,0:T(8,128)(2,1)S(1)} %get-tuple-element.59.refs_0_, bf16[2,256,256]{2,1,0:T(8,128)(2,1)S(1)} %copy-done, f32[224,256]{1,0:T(8,128)S(1)} %get-tuple-element.60.refs_2_, f32[224,256]{1,0:T(8,128)S(1)} %collective-permute-done.7.refs_3_, ...), custom_call_target="tpu_custom_call" | custom-call | tf_op jit(solution)/shard_map/early/pallas_call | solution.py:773
  52.4 12.6 %collective-permute-done.14.refs_5_ = f32[112,256]{1,0:T(8,128)S(1)} collective-permute-done((f32[112,256]{1,0:T(8,128)S(1)}, f32[112,256]{1,0:T(8,128)S(1)}, u32[]{:S(2)}, u32[]{:S(2)}) %collective-permute-start.14) | collective-permute-done | bytes 114720 | tf_op jit(solution)/shard_map/ppermute | solution.py:100
  65.1 0.0 collective-permute-done.12.refs_4_
  65.1 1.3 %late.2.refs_6_ = f32[2,8,128,128]{3,2,1,0:T(8,128)} custom-call(bf16[2,256,192]{2,1,0:T(8,128)(2,1)S(1)} %get-tuple-element.58.refs_0_, bf16[2,256,256]{2,1,0:T(8,128)(2,1)S(1)} %copy-done, f32[8,128,256]{2,1,0:T(8,128)S(1)} %early.1.refs_2_, f32[2,128,128]{2,1,0:T(8,128)S(1)} %get-tuple-element.66.refs_3_, f32[224,256]{1,0:T(8,128)S(1)} %collective-permute-done.12.refs_4_, ...), custom_call_target="tpu_custom_call" | custom-call | tf_op jit(solution)/shard_map/late/pallas_call | solution.py:788
  66.4 0.3 collective-permute-done.13.refs_5_
  66.7 1.3 %late.3 = f32[2,8,128,128]{3,2,1,0:T(8,128)} custom-call(bf16[2,256,192]{2,1,0:T(8,128)(2,1)S(1)} %get-tuple-element.58.refs_0_, bf16[2,256,256]{2,1,0:T(8,128)(2,1)S(1)} %copy-done, f32[8,128,256]{2,1,0:T(8,128)S(1)} %early.1.refs_2_, f32[2,128,128]{2,1,0:T(8,128)S(1)} %get-tuple-element.66.refs_3_, ...), custom_call_target="tpu_custom_call", output_to_operand_aliasing={{}: (6, {})} | custom-call | tf_op jit(solution)/shard_map/late/pallas_call | solution.py:788
  (1 shorter events, 0.0 us)
Async XLA Ops:
  3.3 5.1 %collective-permute-start = (f32[1,72,128]{2,1,0:T(8,128)S(1)}, f32[1,72,128]{2,1,0:T(8,128)S(1)}, u32[]{:S(2)}, u32[]{:S(2)}) collective-permute-start(f32[1,72,128]{2,1,0:T(8,128)S(1)} %get-tuple-element.44.refs_0_), channel_id=1, source_target_pairs={{0,24},{4,28},{8,16},{12,20},{16,8},{20,12},{24,0},{28,4},{1,25},{... | collective-permute-start | bytes 110600 | tf_op jit(solution)/shard_map/ppermute | solution.py:100
  4.9 4.9 %collective-permute-start.1 = (f32[1,72,128]{2,1,0:T(8,128)S(1)}, f32[1,72,128]{2,1,0:T(8,128)S(1)}, u32[]{:S(2)}, u32[]{:S(2)}) collective-permute-start(f32[1,72,128]{2,1,0:T(8,128)S(1)} %get-tuple-element.44.refs_0_), channel_id=1, source_target_pairs={{0,8},{4,12},{8,0},{12,4},{16,24},{20,28},{24,16},{28,20},{1,9},{5... | collective-permute-start | bytes 110600 | tf_op jit(solution)/shard_map/ppermute | solution.py:100
  7.4 4.9 %collective-permute-start.2 = (f32[1,72,128]{2,1,0:T(8,128)S(1)}, f32[1,72,128]{2,1,0:T(8,128)S(1)}, u32[]{:S(2)}, u32[]{:S(2)}) collective-permute-start(f32[1,72,128]{2,1,0:T(8,128)S(1)} %get-tuple-element.44.refs_0_), channel_id=1, source_target_pairs={{0,16},{4,20},{8,24},{12,28},{16,0},{20,4},{24,8},{28,12},{1,17},{... | collective-permute-start | bytes 110600 | tf_op jit(solution)/shard_map/ppermute | solution.py:100
  12.3 7.5 %copy-start.1 = (f32[8,128,256]{2,1,0:T(8,128)S(1)}, f32[8,128,256]{2,1,0:T(8,128)}, u32[]{:S(2)}) copy-start(f32[8,128,256]{2,1,0:T(8,128)} %absorber.1) | copy-start | bytes 3145732
  12.3 5.2 %collective-permute-start.3 = (f32[4,72,128]{2,1,0:T(8,128)S(1)}, f32[4,72,128]{2,1,0:T(8,128)S(1)}, u32[]{:S(2)}, u32[]{:S(2)}) collective-permute-start(f32[4,72,128]{2,1,0:T(8,128)S(1)} %join.1.refs_0_), channel_id=1, source_target_pairs={{0,4},{4,0},{8,12},{12,8},{16,20},{20,16},{24,28},{28,24},{1,5},{5... | collective-permute-start | bytes 442376 | tf_op jit(solution)/shard_map/ppermute | solution.py:100
  17.9 2.4 %collective-permute-start.4 = (f32[40,128]{1,0:T(8,128)S(1)}, f32[40,128]{1,0:T(8,128)S(1)}, u32[]{:S(2)}, u32[]{:S(2)}) collective-permute-start(f32[40,128]{1,0:T(8,128)S(1)} %get-tuple-element.56.refs_5_), channel_id=1, source_target_pairs={{0,1},{1,0},{2,3},{3,2},{4,5},{5,4},{6,7},{7,6},{8,9},{9,8},{10,11... | collective-permute-start | bytes 61448 | tf_op jit(solution)/shard_map/ppermute | solution.py:100
  17.9 3.8 %collective-permute-start.5 = (f32[40,128]{1,0:T(8,128)S(1)}, f32[40,128]{1,0:T(8,128)S(1)}, u32[]{:S(2)}, u32[]{:S(2)}) collective-permute-start(f32[40,128]{1,0:T(8,128)S(1)} %get-tuple-element.56.refs_5_), channel_id=1, source_target_pairs={{0,2},{1,3},{2,0},{3,1},{4,6},{5,7},{6,4},{7,5},{8,10},{9,11},{10,... | collective-permute-start | bytes 61448 | tf_op jit(solution)/shard_map/ppermute | solution.py:100
  19.5 3.2 %collective-permute-start.6 = (f32[40,128]{1,0:T(8,128)S(1)}, f32[40,128]{1,0:T(8,128)S(1)}, u32[]{:S(2)}, u32[]{:S(2)}) collective-permute-start(f32[40,128]{1,0:T(8,128)S(1)} %get-tuple-element.56.refs_5_), channel_id=1, source_target_pairs={{0,3},{1,2},{2,1},{3,0},{4,7},{5,6},{6,5},{7,4},{8,11},{9,10},{10,... | collective-permute-start | bytes 61448 | tf_op jit(solution)/shard_map/ppermute | solution.py:100
  20.3 27.2 %copy-start.2 = (bf16[2,256,128]{2,1,0:T(8,128)(2,1)S(1)}, bf16[2,256,128]{2,1,0:T(8,128)(2,1)}, u32[]{:S(2)}) copy-start(bf16[2,256,128]{2,1,0:T(8,128)(2,1)} %constant.4.clone.refs_2_) | copy-start | bytes 393220
  20.3 27.2 %copy-start.3 = (f32[128,128]{1,0:T(8,128)S(1)}, f32[128,128]{1,0:T(8,128)}, u32[]{:S(2)}) copy-start(f32[128,128]{1,0:T(8,128)} %refs_3_.1) | copy-start | bytes 196612
  20.3 27.2 %copy-start.4 = (s32[1,8,56]{2,1,0:T(8,128)S(1)}, s32[1,8,56]{2,1,0:T(8,128)}, u32[]{:S(2)}) copy-start(s32[1,8,56]{2,1,0:T(8,128)} %param.15) | copy-start | bytes 5380
  20.3 27.2 %copy-start.5 = (s32[1,8,56,1]{2,3,1,0:T(1,128)S(1)}, s32[1,8,56,1]{2,3,1,0:T(1,128)}, u32[]{:S(2)}) copy-start(s32[1,8,56,1]{2,3,1,0:T(1,128)} %param.16) | copy-start | bytes 5380
  24.0 15.4 %collective-permute-start.10 = (f32[224,256]{1,0:T(8,128)S(1)}, f32[224,256]{1,0:T(8,128)S(1)}, u32[]{:S(2)}, u32[]{:S(2)}) collective-permute-start(f32[224,256]{1,0:T(8,128)S(1)} %get-tuple-element.64), channel_id=1, source_target_pairs={{0,16},{4,20},{8,24},{12,28},{16,0},{20,4},{24,8},{28,12},{1,17},{... | collective-permute-start | bytes 688136 | tf_op jit(solution)/shard_map/ppermute | solution.py:100
  24.4 20.2 %collective-permute-start.11 = (f32[224,256]{1,0:T(8,128)S(1)}, f32[224,256]{1,0:T(8,128)S(1)}, u32[]{:S(2)}, u32[]{:S(2)}) collective-permute-start(f32[224,256]{1,0:T(8,128)S(1)} %get-tuple-element.65), channel_id=1, source_target_pairs={{0,20},{4,16},{8,28},{12,24},{16,4},{20,0},{24,12},{28,8},{1,21},{... | collective-permute-start | bytes 688136 | tf_op jit(solution)/shard_map/ppermute | solution.py:100
  27.9 19.4 %collective-permute-start.7 = (f32[224,256]{1,0:T(8,128)S(1)}, f32[224,256]{1,0:T(8,128)S(1)}, u32[]{:S(2)}, u32[]{:S(2)}) collective-permute-start(f32[224,256]{1,0:T(8,128)S(1)} %get-tuple-element.61), channel_id=1, source_target_pairs={{0,4},{4,0},{8,12},{12,8},{16,20},{20,16},{24,28},{28,24},{1,5},{5... | collective-permute-start | bytes 688136 | tf_op jit(solution)/shard_map/ppermute | solution.py:100
  28.4 22.3 %collective-permute-start.8 = (f32[224,256]{1,0:T(8,128)S(1)}, f32[224,256]{1,0:T(8,128)S(1)}, u32[]{:S(2)}, u32[]{:S(2)}) collective-permute-start(f32[224,256]{1,0:T(8,128)S(1)} %get-tuple-element.62), channel_id=1, source_target_pairs={{0,8},{4,12},{8,0},{12,4},{16,24},{20,28},{24,16},{28,20},{1,9},{5... | collective-permute-start | bytes 688136 | tf_op jit(solution)/shard_map/ppermute | solution.py:100
  28.6 22.2 %collective-permute-start.9 = (f32[224,256]{1,0:T(8,128)S(1)}, f32[224,256]{1,0:T(8,128)S(1)}, u32[]{:S(2)}, u32[]{:S(2)}) collective-permute-start(f32[224,256]{1,0:T(8,128)S(1)} %get-tuple-element.63), channel_id=1, source_target_pairs={{0,12},{4,8},{8,4},{12,0},{16,28},{20,24},{24,20},{28,16},{1,13},{... | collective-permute-start | bytes 688136 | tf_op jit(solution)/shard_map/ppermute | solution.py:100
  39.4 25.7 %collective-permute-start.12 = (f32[224,256]{1,0:T(8,128)S(1)}, f32[224,256]{1,0:T(8,128)S(1)}, u32[]{:S(2)}, u32[]{:S(2)}) collective-permute-start(f32[224,256]{1,0:T(8,128)S(1)} %get-tuple-element.67), channel_id=1, source_target_pairs={{0,24},{4,28},{8,16},{12,20},{16,8},{20,12},{24,0},{28,4},{1,25},{... | collective-permute-start | bytes 688136 | tf_op jit(solution)/shard_map/ppermute | solution.py:100
  44.6 20.5 %collective-permute-start.14 = (f32[112,256]{1,0:T(8,128)S(1)}, f32[112,256]{1,0:T(8,128)S(1)}, u32[]{:S(2)}, u32[]{:S(2)}) collective-permute-start(f32[112,256]{1,0:T(8,128)S(1)} %get-tuple-element.69), channel_id=1, source_target_pairs={{0,28},{4,24},{8,20},{12,16},{16,12},{20,8},{24,4},{28,0},{1,29},{... | collective-permute-start | bytes 344072 | tf_op jit(solution)/shard_map/ppermute | solution.py:100
  47.3 19.4 %collective-permute-start.13 = (f32[112,256]{1,0:T(8,128)S(1)}, f32[112,256]{1,0:T(8,128)S(1)}, u32[]{:S(2)}, u32[]{:S(2)}) collective-permute-start(f32[112,256]{1,0:T(8,128)S(1)} %get-tuple-element.68), channel_id=1, source_target_pairs={{0,28},{4,24},{8,20},{12,16},{16,12},{20,8},{24,4},{28,0},{1,29},{... | collective-permute-start | bytes 344072 | tf_op jit(solution)/shard_map/ppermute | solution.py:100
  49.1 1.7 %copy-start = (bf16[2,256,256]{2,1,0:T(8,128)(2,1)S(1)}, bf16[2,256,256]{2,1,0:T(8,128)(2,1)}, u32[]{:S(2)}) copy-start(bf16[2,256,256]{2,1,0:T(8,128)(2,1)} %constant.5.clone.refs_1_) | copy-start | bytes 786436

commit v3 on v2

--- a/solution.py
+++ b/solution.py
@@ -380,7 +380,7 @@
                 there = (n == listed[pl.ds(g, 1), :] * BY + b).astype(f32).astype(bf16)
                 total = total + mm(here.astype(bf16), there, NT)
             q[place * rows : (place + 1) * rows, :] = total
-        cut = (groups - late_of(groups)) * rows
+        cut = (groups - late_of()) * rows
         first = q[0:cut, :].astype(bf16)
         last = q[cut : groups * rows, :].astype(bf16)
         for part in range(2):
@@ -550,8 +550,8 @@
         copy.wait()
 
 
-def late_of(groups):
-    return min(2, groups - 1)
+def late_of():
+    return 1
 
 
 def steps_of(groups):
@@ -735,7 +735,7 @@
         name="lost",
     )(s, spk, kept, bm, place, *edges)
 
-    late = late_of(groups)
+    late = late_of()
     got = [sent[0]] + [exchange(sent[step], step, groups) for step in order[:-1]]
     lasts = [exchange(part, order[-1], groups) for part in [sent[order[-1]]] + sent[groups:]]
 

time: 68.2 us -> 71.2 us (1.044)
  the two profiles are of different devices: /device:TPU:8 before, /device:TPU:16 now
where the time goes in v3:
time: 71.2 us; the launch traced here: 71.1 us
  waiting for transfers between devices  27.6 us (39%)
  starting transfers between devices  26.4 us (37%)
  Pallas kernels  16.2 us (23%)
  between operations  0.84 us (1%)
    ppermute x15, waiting for transfers between devices, exchange(): return lax.ppermute(value, axis, pairs)  27.6 us
    ppermute x15, starting transfers between devices, exchange(): return lax.ppermute(value, axis, pairs)  26.4 us
    pallas_call x1, Pallas kernels, body(): pl.pallas_call(row_edges_kernel, in_specs=[AN] * 6, out_specs=[VM] * 7, o...  2.65 us
    pallas_call x2, Pallas kernels, body(): pl.pallas_call(lambda *refs, first=first: late_kernel(*refs, tail=tail, f...  2.62 us
    pallas_call x1, Pallas kernels, body(): pl.pallas_call(solve_columns_kernel, in_specs=[VM] * 4, out_specs=[VM] *...  2.12 us
    pallas_call x1, Pallas kernels, body(): pl.pallas_call(lambda *refs: early_kernel(*refs, tail=tail), in_specs=[VM...  1.92 us
    pallas_call x1, Pallas kernels, body(): pl.pallas_call(lambda *refs: table_kernel(*refs, tail=tail, norm=norm), i...  1.68 us
    pallas_call x1, Pallas kernels, body(): pl.pallas_call(damp_kernel, in_specs=[VM] * 4, out_specs=AN, out_shape=sd...  1.66 us
  transfers between devices with their start and end apart: 15, of which 7 were waited for; matrix products, arithmetic and copies ran while one was open for 0% of the time, Pallas kernels for 15%

profile of v3, /device:TPU:16, one launch (start us, length us, event | category | flops | bytes accessed | tf_op | source)
XLA Modules:
  0.0 71.1 jit_solution(12672089800214855224)
XLA Ops:
  0.6 2.6 %row_edges.1 = (f32[1,72,128]{2,1,0:T(8,128)S(1)}, f32[8,128]{1,0:T(8,128)S(1)}, f32[2,8,128,256]{3,2,1,0:T(8,128)S(1)}, f32[2,128,128]{2,1,0:T(8,128)S(1)}, f32...) custom-call(f32[2,2,2]{2,1,0:T(2,128)} %terms.1, f32[2,8,128,256]{3,2,1,0:T(8,128)} %w.1, ...), custom_call_target="tpu_custom_call" | custom-call | tf_op jit(solution)/shard_map/row_edges/pallas_call | solution.py:610
  3.3 0.5 collective-permute-start
  3.8 1.2 %collective-permute-start.1 = (f32[1,72,128]{2,1,0:T(8,128)S(1)}, f32[1,72,128]{2,1,0:T(8,128)S(1)}, u32[]{:S(2)}, u32[]{:S(2)}) collective-permute-start(f32[1,72,128]{2,1,0:T(8,128)S(1)} %get-tuple-element.44.refs_0_), channel_id=1, source_target_pairs={{0,8},{4,12},{8,0},{12,4},{16,24},{20,28},{24,16},{28,20},{1,9},{5... | collective-permute-start | bytes 110600 | tf_op jit(solution)/shard_map/ppermute | solution.py:100
  5.0 2.3 %collective-permute-start.2 = (f32[1,72,128]{2,1,0:T(8,128)S(1)}, f32[1,72,128]{2,1,0:T(8,128)S(1)}, u32[]{:S(2)}, u32[]{:S(2)}) collective-permute-start(f32[1,72,128]{2,1,0:T(8,128)S(1)} %get-tuple-element.44.refs_0_), channel_id=1, source_target_pairs={{0,16},{4,20},{8,24},{12,28},{16,0},{20,4},{24,8},{28,12},{1,17},{... | collective-permute-start | bytes 110600 | tf_op jit(solution)/shard_map/ppermute | solution.py:100
  7.3 1.0 %solve_rows.1 = (bf16[1024,512]{1,0:T(8,128)(2,1)S(1)}, bf16[1024,512]{1,0:T(8,128)(2,1)S(1)}) custom-call(f32[2,8,128,256]{3,2,1,0:T(8,128)S(1)} %get-tuple-element.36.w, f32[2,128,128]{2,1,0:T(8,128)S(1)} %get-tuple-element.37.y), custom_call_target="tpu_custom_call" | custom-call | tf_op jit(solution)/shard_map/solve_rows/pallas_call | solution.py:644
  8.3 0.0 collective-permute-done.refs_4_.refs_3_
  8.3 0.0 collective-permute-done.1.refs_1_
  8.3 1.7 %collective-permute-done.2.refs_2_ = f32[1,72,128]{2,1,0:T(8,128)S(1)} collective-permute-done((f32[1,72,128]{2,1,0:T(8,128)S(1)}, f32[1,72,128]{2,1,0:T(8,128)S(1)}, u32[]{:S(2)}, u32[]{:S(2)}) %collective-permute-start.2) | collective-permute-done | bytes 36896 | tf_op jit(solution)/shard_map/ppermute | solution.py:100
  10.1 0.0 copy-start.1
  10.1 1.6 %collective-permute-start.3 = (f32[4,72,128]{2,1,0:T(8,128)S(1)}, f32[4,72,128]{2,1,0:T(8,128)S(1)}, u32[]{:S(2)}, u32[]{:S(2)}) collective-permute-start(f32[4,72,128]{2,1,0:T(8,128)S(1)} %join.1.refs_0_), channel_id=1, source_target_pairs={{0,4},{4,0},{8,12},{12,8},{16,20},{20,16},{24,28},{28,24},{1,5},{5... | collective-permute-start | bytes 442376 | tf_op jit(solution)/shard_map/ppermute | solution.py:100
  11.7 0.4 prepare.1
  12.1 2.1 %solve_columns.1 = (f32[1024,512]{1,0:T(8,128)S(1)}, f32[32,128]{1,0:T(8,128)S(1)}) custom-call(bf16[1024,512]{1,0:T(8,128)(2,1)S(1)} %get-tuple-element.38.th.refs_4_, bf16[1024,512]{1,0:T(8,128)(2,1)S(1)} %get-tuple-element.39.tl, bf16[512,512]{1,0:T(8,128)(2,1)S(1)} %get-tuple-element.45.zh, bf16[512,512]{1,0:T(8,128)(2,1)S(1)} %get-tuple-element.46.zl), custom_call_target="tpu_custom_call" | custom-call | tf_op jit(solution)/shard_map/solve_columns/pallas_call | solution.py:684
  14.2 1.1 %collective-permute-done.3.refs_1_ = f32[4,72,128]{2,1,0:T(8,128)S(1)} collective-permute-done((f32[4,72,128]{2,1,0:T(8,128)S(1)}, f32[4,72,128]{2,1,0:T(8,128)S(1)}, u32[]{:S(2)}, u32[]{:S(2)}) %collective-permute-start.3) | collective-permute-done | bytes 147488 | tf_op jit(solution)/shard_map/ppermute | solution.py:100
  15.3 0.3 row_chain.1
  15.6 0.1 collective-permute-start.4
  15.7 1.6 %collective-permute-start.5 = (f32[40,128]{1,0:T(8,128)S(1)}, f32[40,128]{1,0:T(8,128)S(1)}, u32[]{:S(2)}, u32[]{:S(2)}) collective-permute-start(f32[40,128]{1,0:T(8,128)S(1)} %get-tuple-element.56.refs_5_), channel_id=1, source_target_pairs={{0,2},{1,3},{2,0},{3,1},{4,6},{5,7},{6,4},{7,5},{8,10},{9,11},{10,... | collective-permute-start | bytes 61448 | tf_op jit(solution)/shard_map/ppermute | solution.py:100
  17.3 0.3 collective-permute-start.6
  17.6 0.0 copy-done.1
  17.6 0.5 ready.1
  18.0 0.0 copy-start.2
  18.1 0.0 copy-start.3
  18.1 0.0 copy-start.4
  18.1 0.0 copy-start.5
  18.1 0.0 collective-permute-done.4.refs_6_
  18.1 1.5 %collective-permute-done.5.refs_7_ = f32[40,128]{1,0:T(8,128)S(1)} collective-permute-done((f32[40,128]{1,0:T(8,128)S(1)}, f32[40,128]{1,0:T(8,128)S(1)}, u32[]{:S(2)}, u32[]{:S(2)}) %collective-permute-start.5) | collective-permute-done | bytes 20512 | tf_op jit(solution)/shard_map/ppermute | solution.py:100
  19.6 0.9 %collective-permute-done.6.refs_8_ = f32[40,128]{1,0:T(8,128)S(1)} collective-permute-done((f32[40,128]{1,0:T(8,128)S(1)}, f32[40,128]{1,0:T(8,128)S(1)}, u32[]{:S(2)}, u32[]{:S(2)}) %collective-permute-start.6) | collective-permute-done | bytes 20512 | tf_op jit(solution)/shard_map/ppermute | solution.py:100
  20.5 1.3 %lost.1 = (f32[224,256]{1,0:T(8,128)S(1)}, f32[224,256]{1,0:T(8,128)S(1)}, f32[224,256]{1,0:T(8,128)S(1)}, f32[224,256]{1,0:T(8,128)S(1)}, f32[224,256]{1,0:T(8,...) custom-call(f32[1024,512]{1,0:T(8,128)S(1)} %get-tuple-element.47.re, ...), custom_call_target="tpu_custom_call" | custom-call | tf_op jit(solution)/shard_map/lost/pallas_call | solution.py:723
  21.7 2.4 %collective-permute-start.10 = (f32[224,256]{1,0:T(8,128)S(1)}, f32[224,256]{1,0:T(8,128)S(1)}, u32[]{:S(2)}, u32[]{:S(2)}) collective-permute-start(f32[224,256]{1,0:T(8,128)S(1)} %get-tuple-element.64), channel_id=1, source_target_pairs={{0,16},{4,20},{8,24},{12,28},{16,0},{20,4},{24,8},{28,12},{1,17},{... | collective-permute-start | bytes 688136 | tf_op jit(solution)/shard_map/ppermute | solution.py:100
  24.1 1.6 %collective-permute-start.11 = (f32[224,256]{1,0:T(8,128)S(1)}, f32[224,256]{1,0:T(8,128)S(1)}, u32[]{:S(2)}, u32[]{:S(2)}) collective-permute-start(f32[224,256]{1,0:T(8,128)S(1)} %get-tuple-element.65), channel_id=1, source_target_pairs={{0,20},{4,16},{8,28},{12,24},{16,4},{20,0},{24,12},{28,8},{1,21},{... | collective-permute-start | bytes 688136 | tf_op jit(solution)/shard_map/ppermute | solution.py:100
  25.7 2.7 %collective-permute-start.12 = (f32[224,256]{1,0:T(8,128)S(1)}, f32[224,256]{1,0:T(8,128)S(1)}, u32[]{:S(2)}, u32[]{:S(2)}) collective-permute-start(f32[224,256]{1,0:T(8,128)S(1)} %get-tuple-element.66), channel_id=1, source_target_pairs={{0,24},{4,28},{8,16},{12,20},{16,8},{20,12},{24,0},{28,4},{1,25},{... | collective-permute-start | bytes 688136 | tf_op jit(solution)/shard_map/ppermute | solution.py:100
  28.3 0.5 collective-permute-start.7
  28.9 1.1 %collective-permute-start.8 = (f32[224,256]{1,0:T(8,128)S(1)}, f32[224,256]{1,0:T(8,128)S(1)}, u32[]{:S(2)}, u32[]{:S(2)}) collective-permute-start(f32[224,256]{1,0:T(8,128)S(1)} %get-tuple-element.62), channel_id=1, source_target_pairs={{0,8},{4,12},{8,0},{12,4},{16,24},{20,28},{24,16},{28,20},{1,9},{5... | collective-permute-start | bytes 688136 | tf_op jit(solution)/shard_map/ppermute | solution.py:100
  30.0 14.9 %collective-permute-done.10.refs_6_ = f32[224,256]{1,0:T(8,128)S(1)} collective-permute-done((f32[224,256]{1,0:T(8,128)S(1)}, f32[224,256]{1,0:T(8,128)S(1)}, u32[]{:S(2)}, u32[]{:S(2)}) %collective-permute-start.10) | collective-permute-done | bytes 229408 | tf_op jit(solution)/shard_map/ppermute | solution.py:100
  44.8 2.7 %collective-permute-start.9 = (f32[224,256]{1,0:T(8,128)S(1)}, f32[224,256]{1,0:T(8,128)S(1)}, u32[]{:S(2)}, u32[]{:S(2)}) collective-permute-start(f32[224,256]{1,0:T(8,128)S(1)} %get-tuple-element.63), channel_id=1, source_target_pairs={{0,12},{4,8},{8,4},{12,0},{16,28},{20,24},{24,20},{28,16},{1,13},{... | collective-permute-start | bytes 688136 | tf_op jit(solution)/shard_map/ppermute | solution.py:100
  47.6 2.2 %collective-permute-done.11.refs_7_ = f32[224,256]{1,0:T(8,128)S(1)} collective-permute-done((f32[224,256]{1,0:T(8,128)S(1)}, f32[224,256]{1,0:T(8,128)S(1)}, u32[]{:S(2)}, u32[]{:S(2)}) %collective-permute-start.11) | collective-permute-done | bytes 229408 | tf_op jit(solution)/shard_map/ppermute | solution.py:100
  49.8 0.8 %collective-permute-start.14 = (f32[112,256]{1,0:T(8,128)S(1)}, f32[112,256]{1,0:T(8,128)S(1)}, u32[]{:S(2)}, u32[]{:S(2)}) collective-permute-start(f32[112,256]{1,0:T(8,128)S(1)} %get-tuple-element.69), channel_id=1, source_target_pairs={{0,28},{4,24},{8,20},{12,16},{16,12},{20,8},{24,4},{28,0},{1,29},{... | collective-permute-start | bytes 344072 | tf_op jit(solution)/shard_map/ppermute | solution.py:100
  50.6 5.3 %collective-permute-done.12.refs_8_ = f32[224,256]{1,0:T(8,128)S(1)} collective-permute-done((f32[224,256]{1,0:T(8,128)S(1)}, f32[224,256]{1,0:T(8,128)S(1)}, u32[]{:S(2)}, u32[]{:S(2)}) %collective-permute-start.12) | collective-permute-done | bytes 229408 | tf_op jit(solution)/shard_map/ppermute | solution.py:100
  55.9 7.2 %collective-permute-start.13 = (f32[112,256]{1,0:T(8,128)S(1)}, f32[112,256]{1,0:T(8,128)S(1)}, u32[]{:S(2)}, u32[]{:S(2)}) collective-permute-start(f32[112,256]{1,0:T(8,128)S(1)} %get-tuple-element.68), channel_id=1, source_target_pairs={{0,28},{4,24},{8,20},{12,16},{16,12},{20,8},{24,4},{28,0},{1,29},{... | collective-permute-start | bytes 344072 | tf_op jit(solution)/shard_map/ppermute | solution.py:100
  63.1 0.0 copy-done.2
  63.1 0.0 copy-done.3
  63.1 0.0 copy-done.4
  63.1 0.0 copy-done.5
  63.1 1.7 %tables.1 = (bf16[2,2,256,224]{3,2,1,0:T(8,128)(2,1)S(1)}, bf16[2,256,96]{2,1,0:T(8,128)(2,1)S(1)}, f32[2,128,128]{2,1,0:T(8,128)S(1)}) custom-call(s32[8,56]{1,0:T(8,128)S(1)} %bitcast.3, s32[8,56]{1,0:T(8,128)S(1)} %bitcast.5, bf16[2,256,128]{2,1,0:T(8,128)(2,1)S(1)} %copy-done.2, f32[128,128]{1,0:T(8,128)S(1)} %copy-done.3), custom_call_target="tpu_custom_call" | custom-call | tf_op jit(solution)/shard_map/tables/pallas_call | solution.py:742
  64.8 0.0 copy-start
  64.8 1.7 %damp.1 = f32[2,8,128,256]{3,2,1,0:T(8,128)} custom-call(f32[1024,512]{1,0:T(8,128)S(1)} %get-tuple-element.47.refs_0_.s, f32[8,128,256]{2,1,0:T(8,128)S(1)} %get-tuple-element.53.refs_2_.keep_part, bf16[8,32,128]{2,1,0:T(8,128)(2,1)S(1)} %get-tuple-element.57.am, bf16[8,32,512]{2,1,0:T(8,128)(2,1)S(1)} %get-tuple-element.54.refs_3_.bm), custom_call_target="tpu_custom_call" | custom-call | tf_op jit(solution)/shard_map/damp/pallas_call | solution.py:760
  66.4 0.0 collective-permute-done.7.refs_3_
  66.4 0.0 collective-permute-done.8.refs_4_
  66.5 0.0 collective-permute-done.9.refs_5_
  66.5 0.0 copy-done
  66.5 1.9 %early.1.refs_2_ = f32[8,128,256]{2,1,0:T(8,128)S(1)} custom-call(bf16[2,2,256,224]{3,2,1,0:T(8,128)(2,1)S(1)} %get-tuple-element.59.refs_0_, bf16[2,256,256]{2,1,0:T(8,128)(2,1)S(1)} %copy-done, f32[224,256]{1,0:T(8,128)S(1)} %get-tuple-element.60.refs_2_, f32[224,256]{1,0:T(8,128)S(1)} %collective-permute-done.7.refs_3_, ...), custom_call_target="tpu_custom_call" | custom-call | tf_op jit(solution)/shard_map/early/pallas_call | solution.py:773
  68.4 0.0 collective-permute-done.14.refs_4_
  68.4 1.3 %late.2.refs_5_ = f32[2,8,128,128]{3,2,1,0:T(8,128)} custom-call(bf16[2,256,96]{2,1,0:T(8,128)(2,1)S(1)} %get-tuple-element.58.refs_0_, bf16[2,256,256]{2,1,0:T(8,128)(2,1)S(1)} %copy-done, f32[8,128,256]{2,1,0:T(8,128)S(1)} %early.1.refs_2_, f32[2,128,128]{2,1,0:T(8,128)S(1)} %get-tuple-element.67.refs_3_, f32[112,256]{1,0:T(8,128)S(1)} %collective-permute-done.14.refs_4_), custom_call_target="tpu_custom_call" | custom-call | tf_op jit(solution)/shard_map/late/pallas_call | solution.py:788
  69.7 0.0 collective-permute-done.13.refs_4_
  69.7 1.3 %late.3 = f32[2,8,128,128]{3,2,1,0:T(8,128)} custom-call(bf16[2,256,96]{2,1,0:T(8,128)(2,1)S(1)} %get-tuple-element.58.refs_0_, bf16[2,256,256]{2,1,0:T(8,128)(2,1)S(1)} %copy-done, f32[8,128,256]{2,1,0:T(8,128)S(1)} %early.1.refs_2_, f32[2,128,128]{2,1,0:T(8,128)S(1)} %get-tuple-element.67.refs_3_, ...), custom_call_target="tpu_custom_call", output_to_operand_aliasing={{}: (5, {})} | custom-call | tf_op jit(solution)/shard_map/late/pallas_call | solution.py:788
  (1 shorter events, 0.0 us)
Async XLA Ops:
  3.3 5.0 %collective-permute-start = (f32[1,72,128]{2,1,0:T(8,128)S(1)}, f32[1,72,128]{2,1,0:T(8,128)S(1)}, u32[]{:S(2)}, u32[]{:S(2)}) collective-permute-start(f32[1,72,128]{2,1,0:T(8,128)S(1)} %get-tuple-element.44.refs_0_), channel_id=1, source_target_pairs={{0,24},{4,28},{8,16},{12,20},{16,8},{20,12},{24,0},{28,4},{1,25},{... | collective-permute-start | bytes 110600 | tf_op jit(solution)/shard_map/ppermute | solution.py:100
  3.8 4.5 %collective-permute-start.1 = (f32[1,72,128]{2,1,0:T(8,128)S(1)}, f32[1,72,128]{2,1,0:T(8,128)S(1)}, u32[]{:S(2)}, u32[]{:S(2)}) collective-permute-start(f32[1,72,128]{2,1,0:T(8,128)S(1)} %get-tuple-element.44.refs_0_), channel_id=1, source_target_pairs={{0,8},{4,12},{8,0},{12,4},{16,24},{20,28},{24,16},{28,20},{1,9},{5... | collective-permute-start | bytes 110600 | tf_op jit(solution)/shard_map/ppermute | solution.py:100
  5.0 5.1 %collective-permute-start.2 = (f32[1,72,128]{2,1,0:T(8,128)S(1)}, f32[1,72,128]{2,1,0:T(8,128)S(1)}, u32[]{:S(2)}, u32[]{:S(2)}) collective-permute-start(f32[1,72,128]{2,1,0:T(8,128)S(1)} %get-tuple-element.44.refs_0_), channel_id=1, source_target_pairs={{0,16},{4,20},{8,24},{12,28},{16,0},{20,4},{24,8},{28,12},{1,17},{... | collective-permute-start | bytes 110600 | tf_op jit(solution)/shard_map/ppermute | solution.py:100
  10.1 7.5 %copy-start.1 = (f32[8,128,256]{2,1,0:T(8,128)S(1)}, f32[8,128,256]{2,1,0:T(8,128)}, u32[]{:S(2)}) copy-start(f32[8,128,256]{2,1,0:T(8,128)} %absorber.1) | copy-start | bytes 3145732
  10.1 5.2 %collective-permute-start.3 = (f32[4,72,128]{2,1,0:T(8,128)S(1)}, f32[4,72,128]{2,1,0:T(8,128)S(1)}, u32[]{:S(2)}, u32[]{:S(2)}) collective-permute-start(f32[4,72,128]{2,1,0:T(8,128)S(1)} %join.1.refs_0_), channel_id=1, source_target_pairs={{0,4},{4,0},{8,12},{12,8},{16,20},{20,16},{24,28},{28,24},{1,5},{5... | collective-permute-start | bytes 442376 | tf_op jit(solution)/shard_map/ppermute | solution.py:100
  15.6 2.4 %collective-permute-start.4 = (f32[40,128]{1,0:T(8,128)S(1)}, f32[40,128]{1,0:T(8,128)S(1)}, u32[]{:S(2)}, u32[]{:S(2)}) collective-permute-start(f32[40,128]{1,0:T(8,128)S(1)} %get-tuple-element.56.refs_5_), channel_id=1, source_target_pairs={{0,1},{1,0},{2,3},{3,2},{4,5},{5,4},{6,7},{7,6},{8,9},{9,8},{10,11... | collective-permute-start | bytes 61448 | tf_op jit(solution)/shard_map/ppermute | solution.py:100
  15.7 3.8 %collective-permute-start.5 = (f32[40,128]{1,0:T(8,128)S(1)}, f32[40,128]{1,0:T(8,128)S(1)}, u32[]{:S(2)}, u32[]{:S(2)}) collective-permute-start(f32[40,128]{1,0:T(8,128)S(1)} %get-tuple-element.56.refs_5_), channel_id=1, source_target_pairs={{0,2},{1,3},{2,0},{3,1},{4,6},{5,7},{6,4},{7,5},{8,10},{9,11},{10,... | collective-permute-start | bytes 61448 | tf_op jit(solution)/shard_map/ppermute | solution.py:100
  17.3 3.2 %collective-permute-start.6 = (f32[40,128]{1,0:T(8,128)S(1)}, f32[40,128]{1,0:T(8,128)S(1)}, u32[]{:S(2)}, u32[]{:S(2)}) collective-permute-start(f32[40,128]{1,0:T(8,128)S(1)} %get-tuple-element.56.refs_5_), channel_id=1, source_target_pairs={{0,3},{1,2},{2,1},{3,0},{4,7},{5,6},{6,5},{7,4},{8,11},{9,10},{10,... | collective-permute-start | bytes 61448 | tf_op jit(solution)/shard_map/ppermute | solution.py:100
  18.0 45.0 %copy-start.2 = (bf16[2,256,128]{2,1,0:T(8,128)(2,1)S(1)}, bf16[2,256,128]{2,1,0:T(8,128)(2,1)}, u32[]{:S(2)}) copy-start(bf16[2,256,128]{2,1,0:T(8,128)(2,1)} %constant.4.clone.refs_2_) | copy-start | bytes 393220
  18.1 45.0 %copy-start.3 = (f32[128,128]{1,0:T(8,128)S(1)}, f32[128,128]{1,0:T(8,128)}, u32[]{:S(2)}) copy-start(f32[128,128]{1,0:T(8,128)} %refs_3_.1) | copy-start | bytes 196612
  18.1 45.0 %copy-start.4 = (s32[1,8,56]{2,1,0:T(8,128)S(1)}, s32[1,8,56]{2,1,0:T(8,128)}, u32[]{:S(2)}) copy-start(s32[1,8,56]{2,1,0:T(8,128)} %param.15) | copy-start | bytes 5380
  18.1 45.0 %copy-start.5 = (s32[1,8,56,1]{2,3,1,0:T(1,128)S(1)}, s32[1,8,56,1]{2,3,1,0:T(1,128)}, u32[]{:S(2)}) copy-start(s32[1,8,56,1]{2,3,1,0:T(1,128)} %param.16) | copy-start | bytes 5380
  21.7 23.1 %collective-permute-start.10 = (f32[224,256]{1,0:T(8,128)S(1)}, f32[224,256]{1,0:T(8,128)S(1)}, u32[]{:S(2)}, u32[]{:S(2)}) collective-permute-start(f32[224,256]{1,0:T(8,128)S(1)} %get-tuple-element.64), channel_id=1, source_target_pairs={{0,16},{4,20},{8,24},{12,28},{16,0},{20,4},{24,8},{28,12},{1,17},{... | collective-permute-start | bytes 688136 | tf_op jit(solution)/shard_map/ppermute | solution.py:100
  24.1 25.7 %collective-permute-start.11 = (f32[224,256]{1,0:T(8,128)S(1)}, f32[224,256]{1,0:T(8,128)S(1)}, u32[]{:S(2)}, u32[]{:S(2)}) collective-permute-start(f32[224,256]{1,0:T(8,128)S(1)} %get-tuple-element.65), channel_id=1, source_target_pairs={{0,20},{4,16},{8,28},{12,24},{16,4},{20,0},{24,12},{28,8},{1,21},{... | collective-permute-start | bytes 688136 | tf_op jit(solution)/shard_map/ppermute | solution.py:100
  25.7 30.2 %collective-permute-start.12 = (f32[224,256]{1,0:T(8,128)S(1)}, f32[224,256]{1,0:T(8,128)S(1)}, u32[]{:S(2)}, u32[]{:S(2)}) collective-permute-start(f32[224,256]{1,0:T(8,128)S(1)} %get-tuple-element.66), channel_id=1, source_target_pairs={{0,24},{4,28},{8,16},{12,20},{16,8},{20,12},{24,0},{28,4},{1,25},{... | collective-permute-start | bytes 688136 | tf_op jit(solution)/shard_map/ppermute | solution.py:100
  28.3 38.1 %collective-permute-start.7 = (f32[224,256]{1,0:T(8,128)S(1)}, f32[224,256]{1,0:T(8,128)S(1)}, u32[]{:S(2)}, u32[]{:S(2)}) collective-permute-start(f32[224,256]{1,0:T(8,128)S(1)} %get-tuple-element.61), channel_id=1, source_target_pairs={{0,4},{4,0},{8,12},{12,8},{16,20},{20,16},{24,28},{28,24},{1,5},{5... | collective-permute-start | bytes 688136 | tf_op jit(solution)/shard_map/ppermute | solution.py:100
  28.9 37.6 %collective-permute-start.8 = (f32[224,256]{1,0:T(8,128)S(1)}, f32[224,256]{1,0:T(8,128)S(1)}, u32[]{:S(2)}, u32[]{:S(2)}) collective-permute-start(f32[224,256]{1,0:T(8,128)S(1)} %get-tuple-element.62), channel_id=1, source_target_pairs={{0,8},{4,12},{8,0},{12,4},{16,24},{20,28},{24,16},{28,20},{1,9},{5... | collective-permute-start | bytes 688136 | tf_op jit(solution)/shard_map/ppermute | solution.py:100
  44.8 21.6 %collective-permute-start.9 = (f32[224,256]{1,0:T(8,128)S(1)}, f32[224,256]{1,0:T(8,128)S(1)}, u32[]{:S(2)}, u32[]{:S(2)}) collective-permute-start(f32[224,256]{1,0:T(8,128)S(1)} %get-tuple-element.63), channel_id=1, source_target_pairs={{0,12},{4,8},{8,4},{12,0},{16,28},{20,24},{24,20},{28,16},{1,13},{... | collective-permute-start | bytes 688136 | tf_op jit(solution)/shard_map/ppermute | solution.py:100
  49.8 18.6 %collective-permute-start.14 = (f32[112,256]{1,0:T(8,128)S(1)}, f32[112,256]{1,0:T(8,128)S(1)}, u32[]{:S(2)}, u32[]{:S(2)}) collective-permute-start(f32[112,256]{1,0:T(8,128)S(1)} %get-tuple-element.69), channel_id=1, source_target_pairs={{0,28},{4,24},{8,20},{12,16},{16,12},{20,8},{24,4},{28,0},{1,29},{... | collective-permute-start | bytes 344072 | tf_op jit(solution)/shard_map/ppermute | solution.py:100
  55.9 13.8 %collective-permute-start.13 = (f32[112,256]{1,0:T(8,128)S(1)}, f32[112,256]{1,0:T(8,128)S(1)}, u32[]{:S(2)}, u32[]{:S(2)}) collective-permute-start(f32[112,256]{1,0:T(8,128)S(1)} %get-tuple-element.68), channel_id=1, source_target_pairs={{0,28},{4,24},{8,20},{12,16},{16,12},{20,8},{24,4},{28,0},{1,29},{... | collective-permute-start | bytes 344072 | tf_op jit(solution)/shard_map/ppermute | solution.py:100
  64.8 1.7 %copy-start = (bf16[2,256,256]{2,1,0:T(8,128)(2,1)S(1)}, bf16[2,256,256]{2,1,0:T(8,128)(2,1)}, u32[]{:S(2)}) copy-start(bf16[2,256,256]{2,1,0:T(8,128)(2,1)} %constant.5.clone.refs_1_) | copy-start | bytes 786436
